TPU v7x, 32 devices: a whole 2x2x4 slice. The times are simulated.
32 devices in a mesh: gx: 4 (over x, core), gy: 8 (over z, y).
Axes of the slice: x: 2, y: 2, z: 4, core: 2. Of those that a mesh axis runs over, the one named last changes fastest.
Arguments:
- populations: float32 [19, 64, 4096], P(None, 'gx', 'gy'), may hold values from 0.5 to 1.5
- tracer: float32 [7, 64, 4096], P(None, 'gx', 'gy'), may hold values from 0.2 to 2
- solid_mask: int32 [64, 4096], P('gx', 'gy'), may hold values 0 or 1
- inflow: int32 [64, 4096], P('gx', 'gy'), may hold values 0 or 1
- wind_profile: float32 [3, 32], replicated, may hold values from -0.12 to 0.12
- emission: float32 [64, 4096], P('gx', 'gy'), may hold values from 0.05 to 0.5
Outputs:
- final_populations: float32 [19, 64, 4096], P(None, 'gx', 'gy')
- final_tracer: float32 [7, 64, 4096], P(None, 'gx', 'gy')
All inputs are finite; a program needn't handle non-finite values. No bound on the sum of `solid_mask` or of `inflow` on one device may be relied on, other than what follows from the above.
Results may differ from a plain program's by a relative error of at most 0.0001.
Values sent between devices are 32-bit elements; how exact they have to be, the bound alone decides.
No kernel may reach another device: no remote copies, remote signals or barrier semaphores. Data moves between devices by JAX's collectives and lax.ppermute only.
A program may use at most 64 MiB of HBM per device.

v0:
```python
import math

import jax
import jax.numpy as jnp
from jax import lax
from jax.sharding import PartitionSpec as P

NZ = 32
STEPS = 4


LATTICE = (
    (0, 0, 0),
    (1, 0, 0),
    (-1, 0, 0),
    (0, 1, 0),
    (0, -1, 0),
    (0, 0, 1),
    (0, 0, -1),
    (1, 1, 0),
    (-1, -1, 0),
    (1, -1, 0),
    (-1, 1, 0),
    (1, 0, 1),
    (-1, 0, -1),
    (1, 0, -1),
    (-1, 0, 1),
    (0, 1, 1),
    (0, -1, -1),
    (0, 1, -1),
    (0, -1, 1),
)
OPPOSITE = (0, 2, 1, 4, 3, 6, 5, 8, 7, 10, 9, 12, 11, 14, 13, 16, 15, 18, 17)
WEIGHTS = (1.0 / 3.0,) + (1.0 / 18.0,) * 6 + (1.0 / 36.0,) * 12
TRACER_LATTICE = LATTICE[:7]
TRACER_OPPOSITE = OPPOSITE[:7]
TRACER_WEIGHTS = (0.25,) + (0.125,) * 6
BASE_RELAX = 0.6
SMAGORINSKY = 0.2
TRACER_RELAX = 0.7


def passed_along(shard, axis, by):
    length = lax.axis_size(axis)
    return lax.ppermute(shard, axis, [(i, (i + by) % length) for i in range(length)])


def projection(index, speed, lattice):
    return sum(
        (lattice[index][axis] * speed[axis] for axis in range(3) if lattice[index][axis] != 0)
    )


def equilibrium(rate, speed, speed_sq, index):
    along = projection(index, speed, LATTICE)
    return rate + 3.0 * along + 4.5 * along * along - 1.5 * speed_sq


def collide(populations, tracer, solid_mask, inflow, wind_profile, emission):
    width = populations.shape[2]
    wind_cells = jnp.tile(wind_profile, (1, width // wind_profile.shape[1]))[:, None, :]
    normal = [populations[k] for k in range(19)]
    density = sum((WEIGHTS[k] * normal[k] for k in range(19)))
    velocity = [
        sum((WEIGHTS[k] * LATTICE[k][axis] * normal[k] for k in range(19) if LATTICE[k][axis] != 0))
        for axis in range(3)
    ]
    speed_sq = velocity[0] * velocity[0] + velocity[1] * velocity[1] + velocity[2] * velocity[2]
    deviation = [normal[k] - equilibrium(density, velocity, speed_sq, k) for k in range(19)]
    contraction = 0.0
    for first in range(3):
        for second in range(first, 3):
            stress = sum(
                (
                    WEIGHTS[k] * LATTICE[k][first] * LATTICE[k][second] * deviation[k]
                    for k in range(19)
                    if LATTICE[k][first] * LATTICE[k][second] != 0
                )
            )
            factor = 1.0 if first == second else 2.0
            contraction = contraction + factor * stress * stress
    relax_time = 0.5 * (
        BASE_RELAX
        + jnp.sqrt(
            BASE_RELAX * BASE_RELAX
            + 18.0 * math.sqrt(2.0) * SMAGORINSKY * SMAGORINSKY * jnp.sqrt(contraction)
        )
    )
    wind_sq = (
        wind_cells[0] * wind_cells[0]
        + wind_cells[1] * wind_cells[1]
        + wind_cells[2] * wind_cells[2]
    )
    is_solid = solid_mask == 1
    is_inflow = inflow == 1
    relaxed = []
    for k in range(19):
        held = equilibrium(1.0, wind_cells, wind_sq, k)
        fluid = normal[k] - deviation[k] / relax_time
        relaxed.append(jnp.where(is_solid, normal[OPPOSITE[k]], jnp.where(is_inflow, held, fluid)))
    amount = [tracer[k] for k in range(7)]
    concentration = sum((TRACER_WEIGHTS[k] * amount[k] for k in range(7)))
    traced = []
    for k in range(7):
        balance = concentration * (1.0 + 4.0 * projection(k, velocity, TRACER_LATTICE))
        updated = amount[k] - (amount[k] - balance) / TRACER_RELAX + emission
        traced.append(
            jnp.where(is_solid, amount[TRACER_OPPOSITE[k]], jnp.where(is_inflow, 0.0, updated))
        )
    return (jnp.stack(relaxed), jnp.stack(traced))


def margin_east_west(pieces, offset):
    first, second, third = pieces
    return passed_along((first, second, third), "gx", offset)


def margin_north_south(pieces, offset):
    first, second, third = pieces
    return passed_along((first, second, third), "gy", offset)


def local_stream(relaxed, lattice, opposite):
    number, extent_x, width = relaxed.shape
    padded = jnp.pad(relaxed, ((0, 0), (1, 1), (NZ + 1, NZ + 1)))
    height = lax.iota(jnp.int32, width) % NZ
    layers = []
    for k in range(number):
        step_x, step_y, step_z = lattice[k]
        offset = 1 + NZ - step_y * NZ - step_z
        shifted = padded[k, 1 - step_x : 1 - step_x + extent_x, offset : offset + width]
        if step_z == 1:
            shifted = jnp.where(height >= 1, shifted, relaxed[opposite[k]])
        elif step_z == -1:
            shifted = jnp.where(height <= NZ - 2, shifted, relaxed[opposite[k]])
        layers.append(shifted)
    return jnp.stack(layers)


def margin_run(populations, tracer, solid_mask, inflow, wind_profile, emission):
    depth = STEPS
    block_x = populations.shape[1]
    width = populations.shape[2]
    fields = jnp.stack([solid_mask.astype(jnp.float32), inflow.astype(jnp.float32), emission])
    pieces = (populations, tracer, fields)
    west_part = margin_east_west(tuple((p[:, block_x - depth :] for p in pieces)), 1)
    east_part = margin_east_west(tuple((p[:, :depth] for p in pieces)), -1)
    wide = tuple((jnp.concatenate([w, p, e], 1) for w, p, e in zip(west_part, pieces, east_part)))
    south_part = margin_north_south(tuple((p[:, :, width - depth * NZ :] for p in wide)), 1)
    north_part = margin_north_south(tuple((p[:, :, : depth * NZ] for p in wide)), -1)
    grown = tuple((jnp.concatenate([s, p, n], 2) for s, p, n in zip(south_part, wide, north_part)))
    flow, amount, cell_fields = grown
    solid_grown = jnp.where(cell_fields[0] == 1.0, 1, 0).astype(jnp.int32)
    inflow_grown = jnp.where(cell_fields[1] == 1.0, 1, 0).astype(jnp.int32)
    for iteration in range(STEPS):
        relaxed, traced = collide(
            flow, amount, solid_grown, inflow_grown, wind_profile, cell_fields[2]
        )
        flow = local_stream(relaxed, LATTICE, OPPOSITE)
        amount = local_stream(traced, TRACER_LATTICE, TRACER_OPPOSITE)
    low = depth * NZ
    return (
        flow[:, depth : depth + block_x, low : low + width],
        amount[:, depth : depth + block_x, low : low + width],
    )


def local(populations, tracer, solid_mask, inflow, wind_profile, emission):
    return margin_run(populations, tracer, solid_mask, inflow, wind_profile, emission)


def solution(mesh):
    in_specs = (
        P(None, "gx", "gy"),
        P(None, "gx", "gy"),
        P("gx", "gy"),
        P("gx", "gy"),
        P(),
        P("gx", "gy"),
    )
    out_specs = (P(None, "gx", "gy"), P(None, "gx", "gy"))
    return jax.shard_map(local, mesh=mesh, in_specs=in_specs, out_specs=out_specs, check_vma=False)
```

profile of v0, /device:TPU:0, one launch (start us, length us, event | category | flops | bytes accessed | tf_op | source)
XLA Modules:
  0.0 59.5 jit_solution(1288204923148525901)
XLA Ops:
  2.8 2.0 %collective-permute-start.1 = (f32[3,4,512]{2,1,0:T(4,128)S(1)}, f32[3,4,512]{2,1,0:T(4,128)S(1)}, u32[]{:S(2)}, u32[]{:S(2)}) collective-permute-start(f32[3,4,512]{2,1,0:T(4,128)S(1)} %get-tuple-element.245), channel_id=1, source_target_pairs={{0,24},{8,0},{16,8},{24,16},{1,25},{9,1},{17,9},{25,17},{2,26},{10... | collective-permute-start | bytes 73736 | tf_op jit(solution)/shard_map/ppermute | solution.py:45
  4.7 1.0 %fusion.483 = (f32[7,4,512]{2,1,0:T(4,128)S(1)}, f32[7,4,512]{2,1,0:T(4,128)S(1)}) fusion(f32[7,16,512]{2,1,0:T(8,128)} %param.7), kind=kLoop, calls=%fused_computation.854 | loop fusion | bytes 229376 | tf_op jit(solution)/shard_map/slice | solution.py:146
  6.4 1.1 %collective-permute-start.9 = (f32[7,4,512]{2,1,0:T(4,128)S(1)}, f32[7,4,512]{2,1,0:T(4,128)S(1)}, u32[]{:S(2)}, u32[]{:S(2)}) collective-permute-start(f32[7,4,512]{2,1,0:T(4,128)S(1)} %get-tuple-element.235), channel_id=1, source_target_pairs={{0,24},{8,0},{16,8},{24,16},{1,25},{9,1},{17,9},{25,17},{2,26},{10... | collective-permute-start | bytes 172040 | tf_op jit(solution)/shard_map/ppermute | solution.py:45
  7.5 1.1 %fusion.482 = (f32[19,4,512]{2,1,0:T(4,128)S(1)}, f32[19,4,512]{2,1,0:T(4,128)S(1)}) fusion(f32[19,16,512]{2,1,0:T(8,128)} %param.6), kind=kLoop, calls=%fused_computation.853 | loop fusion | bytes 622592 | tf_op jit(solution)/shard_map/slice | solution.py:146
  10.5 1.1 %collective-permute-start.5 = (f32[19,4,512]{2,1,0:T(4,128)S(1)}, f32[19,4,512]{2,1,0:T(4,128)S(1)}, u32[]{:S(2)}, u32[]{:S(2)}) collective-permute-start(f32[19,4,512]{2,1,0:T(4,128)S(1)} %get-tuple-element.231), channel_id=1, source_target_pairs={{0,24},{8,0},{16,8},{24,16},{1,25},{9,1},{17,9},{25,17},{2,26},{10... | collective-permute-start | bytes 466952 | tf_op jit(solution)/shard_map/ppermute | solution.py:45
  12.3 2.3 %collective-permute-start.2 = (f32[3,24,128]{2,1,0:T(8,128)S(1)}, f32[3,24,128]{2,1,0:T(8,128)S(1)}, u32[]{:S(2)}, u32[]{:S(2)}) collective-permute-start(f32[3,24,128]{2,1,0:T(8,128)S(1)} %get-tuple-element.236), channel_id=1, source_target_pairs={{0,1},{1,2},{2,3},{3,4},{4,5},{5,6},{6,7},{7,0},{8,9},{9,10},{10,1... | collective-permute-start | bytes 110600 | tf_op jit(solution)/shard_map/ppermute | solution.py:45
  14.7 3.1 %collective-permute-start.3 = (f32[3,24,128]{2,1,0:T(8,128)S(1)}, f32[3,24,128]{2,1,0:T(8,128)S(1)}, u32[]{:S(2)}, u32[]{:S(2)}) collective-permute-start(f32[3,24,128]{2,1,0:T(8,128)S(1)} %get-tuple-element.237), channel_id=1, source_target_pairs={{0,7},{1,0},{2,1},{3,2},{4,3},{5,4},{6,5},{7,6},{8,15},{9,8},{10,9... | collective-permute-start | bytes 110600 | tf_op jit(solution)/shard_map/ppermute | solution.py:45
  17.9 1.8 %collective-permute-done.2 = f32[3,24,128]{2,1,0:T(8,128)S(1)} collective-permute-done((f32[3,24,128]{2,1,0:T(8,128)S(1)}, f32[3,24,128]{2,1,0:T(8,128)S(1)}, u32[]{:S(2)}, u32[]{:S(2)}) %collective-permute-start.2) | collective-permute-done | bytes 36896 | tf_op jit(solution)/shard_map/ppermute | solution.py:45
  19.6 3.0 %collective-permute-start.11 = (f32[7,24,128]{2,1,0:T(8,128)S(1)}, f32[7,24,128]{2,1,0:T(8,128)S(1)}, u32[]{:S(2)}, u32[]{:S(2)}) collective-permute-start(f32[7,24,128]{2,1,0:T(8,128)S(1)} %get-tuple-element.233), channel_id=1, source_target_pairs={{0,7},{1,0},{2,1},{3,2},{4,3},{5,4},{6,5},{7,6},{8,15},{9,8},{10,9... | collective-permute-start | bytes 258056 | tf_op jit(solution)/shard_map/ppermute | solution.py:45
  22.6 2.4 %collective-permute-done.10 = f32[7,24,128]{2,1,0:T(8,128)S(1)} collective-permute-done((f32[7,24,128]{2,1,0:T(8,128)S(1)}, f32[7,24,128]{2,1,0:T(8,128)S(1)}, u32[]{:S(2)}, u32[]{:S(2)}) %collective-permute-start.10) | collective-permute-done | bytes 86048 | tf_op jit(solution)/shard_map/ppermute | solution.py:45
  25.8 4.7 %collective-permute-start.7 = (f32[19,24,128]{2,1,0:T(8,128)S(1)}, f32[19,24,128]{2,1,0:T(8,128)S(1)}, u32[]{:S(2)}, u32[]{:S(2)}) collective-permute-start(f32[19,24,128]{2,1,0:T(8,128)S(1)} %get-tuple-element.229), channel_id=1, source_target_pairs={{0,7},{1,0},{2,1},{3,2},{4,3},{5,4},{6,5},{7,6},{8,15},{9,8},{10,9... | collective-permute-start | bytes 700424 | tf_op jit(solution)/shard_map/ppermute | solution.py:45
  30.6 4.0 %collective-permute-done.6 = f32[19,24,128]{2,1,0:T(8,128)S(1)} collective-permute-done((f32[19,24,128]{2,1,0:T(8,128)S(1)}, f32[19,24,128]{2,1,0:T(8,128)S(1)}, u32[]{:S(2)}, u32[]{:S(2)}) %collective-permute-start.6) | collective-permute-done | bytes 233504 | tf_op jit(solution)/shard_map/ppermute | solution.py:45
  34.5 2.1 %collective-permute-done.7 = f32[19,24,128]{2,1,0:T(8,128)S(1)} collective-permute-done((f32[19,24,128]{2,1,0:T(8,128)S(1)}, f32[19,24,128]{2,1,0:T(8,128)S(1)}, u32[]{:S(2)}, u32[]{:S(2)}) %collective-permute-start.7) | collective-permute-done | bytes 233504 | tf_op jit(solution)/shard_map/ppermute | solution.py:45
  38.4 1.0 %constant_dynamic-update-slice_fusion.7 = (f32[19,24,768]{2,1,0:T(8,128)S(1)}, f32[1,24,768]{2,1,0:T(8,128)S(1)}) fusion(f32[19,24,768]{2,1,0:T(8,128)S(1)} %constant_dynamic-update-slice_fusion.8, pred[1,24,768]{2,1,0:T(8,128)(4,1)S(1)} %get-tuple-element.86, pred[1,24,768]{2,1,0:T(8,128)(4,1)S(1)} %get-tuple-element.85, ...), kind=kLoop, calls=%fused_computation.105 | loop fusion | flops 73728 | bytes 483328
  39.4 1.0 %constant_dynamic-update-slice_fusion.6 = (f32[19,24,768]{2,1,0:T(8,128)S(1)}, f32[1,24,768]{2,1,0:T(8,128)S(1)}) fusion(f32[19,24,768]{2,1,0:T(8,128)S(1)} %get-tuple-element.201, pred[1,24,768]{2,1,0:T(8,128)(4,1)S(1)} %get-tuple-element.86, pred[1,24,768]{2,1,0:T(8,128)(4,1)S(1)} %get-tuple-element.85, f32[1,24,768]{2,1,0:T(8,128)S(1)} %get-tuple-element.213, ...), kind=kLoop, calls=%fused_computation.104 | loop fusion | flops 73728 | bytes 483328
  40.3 1.0 %constant_dynamic-update-slice_fusion.5 = (f32[19,24,768]{2,1,0:T(8,128)S(1)}, f32[1,24,768]{2,1,0:T(8,128)S(1)}) fusion(f32[19,24,768]{2,1,0:T(8,128)S(1)} %get-tuple-element.199, pred[1,24,768]{2,1,0:T(8,128)(4,1)S(1)} %get-tuple-element.86, pred[1,24,768]{2,1,0:T(8,128)(4,1)S(1)} %get-tuple-element.85, f32[1,24,768]{2,1,0:T(8,128)S(1)} %get-tuple-element.216, ...), kind=kLoop, calls=%fused_computation.103 | loop fusion | flops 73728 | bytes 483328
  41.3 1.0 %constant_dynamic-update-slice_fusion.4 = (f32[19,24,768]{2,1,0:T(8,128)S(1)}, f32[1,24,768]{2,1,0:T(8,128)S(1)}) fusion(f32[19,24,768]{2,1,0:T(8,128)S(1)} %get-tuple-element.197, pred[1,24,768]{2,1,0:T(8,128)(4,1)S(1)} %get-tuple-element.86, pred[1,24,768]{2,1,0:T(8,128)(4,1)S(1)} %get-tuple-element.85, f32[1,24,768]{2,1,0:T(8,128)S(1)} %get-tuple-element.217, ...), kind=kLoop, calls=%fused_computation.102 | loop fusion | flops 73728 | bytes 483328
  42.2 1.0 %constant_dynamic-update-slice_fusion.3 = (f32[19,24,768]{2,1,0:T(8,128)S(1)}, f32[1,24,768]{2,1,0:T(8,128)S(1)}) fusion(f32[19,24,768]{2,1,0:T(8,128)S(1)} %get-tuple-element.195, pred[1,24,768]{2,1,0:T(8,128)(4,1)S(1)} %get-tuple-element.86, pred[1,24,768]{2,1,0:T(8,128)(4,1)S(1)} %get-tuple-element.85, f32[1,24,768]{2,1,0:T(8,128)S(1)} %get-tuple-element.218, ...), kind=kLoop, calls=%fused_computation.101 | loop fusion | flops 73728 | bytes 483328
  43.2 1.0 %constant_dynamic-update-slice_fusion.2 = (f32[19,24,768]{2,1,0:T(8,128)S(1)}, f32[1,24,768]{2,1,0:T(8,128)S(1)}) fusion(f32[19,24,768]{2,1,0:T(8,128)S(1)} %get-tuple-element.193, pred[1,24,768]{2,1,0:T(8,128)(4,1)S(1)} %get-tuple-element.86, pred[1,24,768]{2,1,0:T(8,128)(4,1)S(1)} %get-tuple-element.85, f32[1,24,768]{2,1,0:T(8,128)S(1)} %get-tuple-element.219, ...), kind=kLoop, calls=%fused_computation.100 | loop fusion | flops 73728 | bytes 483328
  44.2 1.0 %constant_dynamic-update-slice_fusion.1 = (f32[19,24,768]{2,1,0:T(8,128)S(1)}, f32[1,24,768]{2,1,0:T(8,128)S(1)}) fusion(f32[19,24,768]{2,1,0:T(8,128)S(1)} %get-tuple-element.191, pred[1,24,768]{2,1,0:T(8,128)(4,1)S(1)} %get-tuple-element.86, pred[1,24,768]{2,1,0:T(8,128)(4,1)S(1)} %get-tuple-element.85, f32[1,24,768]{2,1,0:T(8,128)S(1)} %get-tuple-element.220, ...), kind=kLoop, calls=%fused_computation.99 | loop fusion | flops 73728 | bytes 483328
  45.1 1.1 %constant_dynamic-update-slice_fusion = (f32[19,24,768]{2,1,0:T(8,128)S(1)}, f32[1,24,768]{2,1,0:T(8,128)S(1)}, f32[7,24,768]{2,1,0:T(8,128)S(1)}, f32[1,24,768]...) fusion(f32[19,24,768]{2,1,0:T(8,128)S(1)} %get-tuple-element.189, ...), kind=kLoop, calls=%fused_computation.98 | loop fusion | flops 460799 | bytes 1665024 | tf_op jit(solution)/shard_map/stack | solution.py:110
  50.4 0.9 %constant_dynamic-update-slice_fusion.56 = (f32[19,24,768]{2,1,0:T(8,128)S(1)}, f32[1,24,768]{2,1,0:T(8,128)S(1)}, f32[1,24,768]{2,1,0:T(8,128)S(1)}, f32[1,24,7...) fusion(pred[1,24,768]{2,1,0:T(8,128)(4,1)S(1)} %get-tuple-eleme, ...), kind=kLoop, calls=%fused_computation.154 | loop fusion | flops 4884479 | bytes 3431424
  53.7 1.0 %select_select_fusion.22 = (f32[1,24,768]{2,1,0:T(8,128)S(1)}, f32[1,24,768]{2,1,0:T(8,128)S(1)}, f32[1,24,768]{2,1,0:T(8,128)S(1)}, f32[1,24,768]{2,1,0:T(8,128...) fusion(pred[1,24,768]{2,1,0:T(8,128)(4,1)S(1)} %get-tuple-eleme, ...), kind=kLoop, calls=%fused_computation.715 | loop fusion | flops 4884480 | bytes 3357696 | tf_op jit(solution)/shard_map/jit(_where)/select_n | solution.py:100
  58.6 0.9 %slice.765 = f32[19,16,512]{2,1,0:T(8,128)} slice(f32[19,24,768]{2,1,0:T(8,128)S(1)} %constant_dynamic-update-slice_fusion.76), slice={[0:19], [4:20], [128:640]} | slice | bytes 1245184 | tf_op jit(solution)/shard_map/slice | solution.py:163
  (154 shorter events, 18.0 us)
Async XLA Ops:
  0.6 22.0 %copy-start.3 = (f32[16,512]{1,0:T(8,128)S(1)}, f32[16,512]{1,0:T(8,128)}, u32[]{:S(2)}) copy-start(f32[16,512]{1,0:T(8,128)} %param.11) | copy-start | bytes 98308
  0.6 17.1 %copy-start.2 = (f32[7,16,512]{2,1,0:T(8,128)S(1)}, f32[7,16,512]{2,1,0:T(8,128)}, u32[]{:S(2)}) copy-start(f32[7,16,512]{2,1,0:T(8,128)} %param.7) | copy-start | bytes 688132
  2.2 8.2 %collective-permute-start = (f32[3,4,512]{2,1,0:T(4,128)S(1)}, f32[3,4,512]{2,1,0:T(4,128)S(1)}, u32[]{:S(2)}, u32[]{:S(2)}) collective-permute-start(f32[3,4,512]{2,1,0:T(4,128)S(1)} %get-tuple-element.244), channel_id=1, source_target_pairs={{0,8},{8,16},{16,24},{24,0},{1,9},{9,17},{17,25},{25,1},{2,10},{10... | collective-permute-start | bytes 73736 | tf_op jit(solution)/shard_map/ppermute | solution.py:45
  2.8 8.8 %collective-permute-start.1 = (f32[3,4,512]{2,1,0:T(4,128)S(1)}, f32[3,4,512]{2,1,0:T(4,128)S(1)}, u32[]{:S(2)}, u32[]{:S(2)}) collective-permute-start(f32[3,4,512]{2,1,0:T(4,128)S(1)} %get-tuple-element.245), channel_id=1, source_target_pairs={{0,24},{8,0},{16,8},{24,16},{1,25},{9,1},{17,9},{25,17},{2,26},{10... | collective-permute-start | bytes 73736 | tf_op jit(solution)/shard_map/ppermute | solution.py:45
  5.7 8.9 %collective-permute-start.8 = (f32[7,4,512]{2,1,0:T(4,128)S(1)}, f32[7,4,512]{2,1,0:T(4,128)S(1)}, u32[]{:S(2)}, u32[]{:S(2)}) collective-permute-start(f32[7,4,512]{2,1,0:T(4,128)S(1)} %get-tuple-element.234), channel_id=1, source_target_pairs={{0,8},{8,16},{16,24},{24,0},{1,9},{9,17},{17,25},{25,1},{2,10},{10... | collective-permute-start | bytes 172040 | tf_op jit(solution)/shard_map/ppermute | solution.py:45
  6.4 19.2 %copy-start.1 = (f32[19,16,512]{2,1,0:T(8,128)S(1)}, f32[19,16,512]{2,1,0:T(8,128)}, u32[]{:S(2)}) copy-start(f32[19,16,512]{2,1,0:T(8,128)} %param.6) | copy-start | bytes 1867780
  6.4 11.4 %collective-permute-start.9 = (f32[7,4,512]{2,1,0:T(4,128)S(1)}, f32[7,4,512]{2,1,0:T(4,128)S(1)}, u32[]{:S(2)}, u32[]{:S(2)}) collective-permute-start(f32[7,4,512]{2,1,0:T(4,128)S(1)} %get-tuple-element.235), channel_id=1, source_target_pairs={{0,24},{8,0},{16,8},{24,16},{1,25},{9,1},{17,9},{25,17},{2,26},{10... | collective-permute-start | bytes 172040 | tf_op jit(solution)/shard_map/ppermute | solution.py:45
  8.7 17.0 %collective-permute-start.4 = (f32[19,4,512]{2,1,0:T(4,128)S(1)}, f32[19,4,512]{2,1,0:T(4,128)S(1)}, u32[]{:S(2)}, u32[]{:S(2)}) collective-permute-start(f32[19,4,512]{2,1,0:T(4,128)S(1)} %get-tuple-element.230), channel_id=1, source_target_pairs={{0,8},{8,16},{16,24},{24,0},{1,9},{9,17},{17,25},{25,1},{2,10},{10... | collective-permute-start | bytes 466952 | tf_op jit(solution)/shard_map/ppermute | solution.py:45
  10.5 15.1 %collective-permute-start.5 = (f32[19,4,512]{2,1,0:T(4,128)S(1)}, f32[19,4,512]{2,1,0:T(4,128)S(1)}, u32[]{:S(2)}, u32[]{:S(2)}) collective-permute-start(f32[19,4,512]{2,1,0:T(4,128)S(1)} %get-tuple-element.231), channel_id=1, source_target_pairs={{0,24},{8,0},{16,8},{24,16},{1,25},{9,1},{17,9},{25,17},{2,26},{10... | collective-permute-start | bytes 466952 | tf_op jit(solution)/shard_map/ppermute | solution.py:45
  12.3 7.3 %collective-permute-start.2 = (f32[3,24,128]{2,1,0:T(8,128)S(1)}, f32[3,24,128]{2,1,0:T(8,128)S(1)}, u32[]{:S(2)}, u32[]{:S(2)}) collective-permute-start(f32[3,24,128]{2,1,0:T(8,128)S(1)} %get-tuple-element.236), channel_id=1, source_target_pairs={{0,1},{1,2},{2,3},{3,4},{4,5},{5,6},{6,7},{7,0},{8,9},{9,10},{10,1... | collective-permute-start | bytes 110600 | tf_op jit(solution)/shard_map/ppermute | solution.py:45
  14.7 7.9 %collective-permute-start.3 = (f32[3,24,128]{2,1,0:T(8,128)S(1)}, f32[3,24,128]{2,1,0:T(8,128)S(1)}, u32[]{:S(2)}, u32[]{:S(2)}) collective-permute-start(f32[3,24,128]{2,1,0:T(8,128)S(1)} %get-tuple-element.237), channel_id=1, source_target_pairs={{0,7},{1,0},{2,1},{3,2},{4,3},{5,4},{6,5},{7,6},{8,15},{9,8},{10,9... | collective-permute-start | bytes 110600 | tf_op jit(solution)/shard_map/ppermute | solution.py:45
  17.8 7.2 %collective-permute-start.10 = (f32[7,24,128]{2,1,0:T(8,128)S(1)}, f32[7,24,128]{2,1,0:T(8,128)S(1)}, u32[]{:S(2)}, u32[]{:S(2)}) collective-permute-start(f32[7,24,128]{2,1,0:T(8,128)S(1)} %get-tuple-element.232), channel_id=1, source_target_pairs={{0,1},{1,2},{2,3},{3,4},{4,5},{5,6},{6,7},{7,0},{8,9},{9,10},{10,1... | collective-permute-start | bytes 258056 | tf_op jit(solution)/shard_map/ppermute | solution.py:45
  19.6 5.9 %collective-permute-start.11 = (f32[7,24,128]{2,1,0:T(8,128)S(1)}, f32[7,24,128]{2,1,0:T(8,128)S(1)}, u32[]{:S(2)}, u32[]{:S(2)}) collective-permute-start(f32[7,24,128]{2,1,0:T(8,128)S(1)} %get-tuple-element.233), channel_id=1, source_target_pairs={{0,7},{1,0},{2,1},{3,2},{4,3},{5,4},{6,5},{7,6},{8,15},{9,8},{10,9... | collective-permute-start | bytes 258056 | tf_op jit(solution)/shard_map/ppermute | solution.py:45
  25.7 8.8 %collective-permute-start.6 = (f32[19,24,128]{2,1,0:T(8,128)S(1)}, f32[19,24,128]{2,1,0:T(8,128)S(1)}, u32[]{:S(2)}, u32[]{:S(2)}) collective-permute-start(f32[19,24,128]{2,1,0:T(8,128)S(1)} %get-tuple-element.228), channel_id=1, source_target_pairs={{0,1},{1,2},{2,3},{3,4},{4,5},{5,6},{6,7},{7,0},{8,9},{9,10},{10,1... | collective-permute-start | bytes 700424 | tf_op jit(solution)/shard_map/ppermute | solution.py:45
  25.8 10.8 %collective-permute-start.7 = (f32[19,24,128]{2,1,0:T(8,128)S(1)}, f32[19,24,128]{2,1,0:T(8,128)S(1)}, u32[]{:S(2)}, u32[]{:S(2)}) collective-permute-start(f32[19,24,128]{2,1,0:T(8,128)S(1)} %get-tuple-element.229), channel_id=1, source_target_pairs={{0,7},{1,0},{2,1},{3,2},{4,3},{5,4},{6,5},{7,6},{8,15},{9,8},{10,9... | collective-permute-start | bytes 700424 | tf_op jit(solution)/shard_map/ppermute | solution.py:45
  36.8 1.6 %copy-start = (f32[19,24,768]{2,1,0:T(8,128)}, f32[19,24,768]{2,1,0:T(8,128)S(1)}, u32[]{:S(2)}) copy-start(f32[19,24,768]{2,1,0:T(8,128)S(1)} %pad_maximum_fusion) | copy-start | bytes 4202500
where the time goes:
time: 60.2 us; the launch traced here: 59.5 us
  other arithmetic  22.5 us (37%)
  starting transfers between devices  19.4 us (32%)
  waiting for transfers between devices  10.7 us (18%)
  local copies, waits for them, and re-layouts  5.62 us (9%)
  between operations  1.37 us (2%)
    ppermute x12, starting transfers between devices, passed_along(): lax.ppermute(shard, axis, [(i, (i + by) % length) for i in range(length)])  19.4 us
    unnamed x99, other arithmetic  17 us
    ppermute x12, waiting for transfers between devices, passed_along(): lax.ppermute(shard, axis, [(i, (i + by) % length) for i in range(length)])  10.7 us
    slice x2, local copies, waits for them, and re-layouts, margin_run(): p[:, block_x - depth:]  2.1 us
    another operation x6, other arithmetic, collide(): return (jnp.stack(relaxed), jnp.stack(traced))  1.61 us
  transfers between devices with their start and end apart: 12, of which 5 were waited for; matrix products, arithmetic and copies ran while one was open for 7% of the time, Pallas kernels for 0%

commit v1 on v0

v1 whole, which is shorter than its diff:
```python
import math

import jax
import jax.numpy as jnp
from jax import lax
from jax.experimental import pallas as pl
from jax.experimental.pallas import tpu as pltpu
from jax.sharding import PartitionSpec as P

STEPS = 4
LANES = 128
ROWS = 8

LATTICE = (
    (0, 0, 0),
    (1, 0, 0),
    (-1, 0, 0),
    (0, 1, 0),
    (0, -1, 0),
    (0, 0, 1),
    (0, 0, -1),
    (1, 1, 0),
    (-1, -1, 0),
    (1, -1, 0),
    (-1, 1, 0),
    (1, 0, 1),
    (-1, 0, -1),
    (1, 0, -1),
    (-1, 0, 1),
    (0, 1, 1),
    (0, -1, -1),
    (0, 1, -1),
    (0, -1, 1),
)
OPPOSITE = (0, 2, 1, 4, 3, 6, 5, 8, 7, 10, 9, 12, 11, 14, 13, 16, 15, 18, 17)
BASE_RELAX = 0.6
SMAGORINSKY = 0.2
TRACER_RELAX = 0.7

FLOW = 19
MOVING = 26
SOLID, INFLOW, EMISSION = 26, 27, 28
UNITS = 29
SPEED = LATTICE + LATTICE[:7] + ((0, 0, 0),) * 3
TURNED = OPPOSITE + tuple(FLOW + k for k in OPPOSITE[:7])


def split_units(axis, sign):
    along = [u for u in range(UNITS) if SPEED[u][axis] == sign]
    still = [u for u in range(UNITS) if SPEED[u][axis] == 0]
    against = [u for u in range(UNITS) if SPEED[u][axis] == -sign]
    return along, still, against


def wall_pair(axis, sign):
    against = split_units(axis, sign)[2]
    return tuple(next(u for u in against if SPEED[u][2] == step) for step in (-1, 1))


def row_plan(sign):
    plan, offset = [], 0
    for units, depth in zip(split_units(0, sign), (STEPS, STEPS - 1, STEPS - 2)):
        for u in units:
            plan.append((u, STEPS - depth if sign > 0 else 0, depth, offset))
            offset += depth
    return plan, (offset, 1 if sign > 0 else 2), -(-(offset + 1) // ROWS) * ROWS


def pack_rows(read, store, sign, first, height):
    plan, (offset, row), _ = row_plan(sign)
    for u, low, depth, at in plan:
        store(at, depth, read(u, first + low, depth))
    floor, roof = wall_pair(0, sign)
    store(offset, 1, jnp.where(height[:1] == 0, read(floor, first + row, 1), read(roof, first + row, 1)))


def unpack_rows(read, store, sign, first):
    plan, (offset, row), _ = row_plan(sign)
    for u, low, depth, at in plan:
        store(u, first + low, read(at, depth))
    for u in wall_pair(0, sign):
        store(u, first + row, read(offset, 1))


def pack_columns(read, store, sign, lane, nz):
    along, still, against = split_units(1, sign)
    for t, u in enumerate(along):
        store(t, read(u))
    half = LANES // 2
    for t, u in enumerate(still):
        value = read(u)
        if t < 2 * len(against):
            chunk = t % 2
            other = read(against[t // 2])
            if sign > 0:
                value = jnp.where(lane < nz, pltpu.roll(other, half - nz * chunk, 1), value)
            else:
                value = jnp.where(lane >= LANES - nz, pltpu.roll(other, LANES - nz - nz * chunk, 1), value)
        elif t == 2 * len(against):
            floor, roof = wall_pair(1, sign)
            other = jnp.where(lane % nz == 0, read(floor), read(roof))
            if sign > 0:
                value = jnp.where(lane < nz, pltpu.roll(other, LANES - nz, 1), value)
            else:
                value = jnp.where(lane >= LANES - nz, pltpu.roll(other, nz, 1), value)
        store(len(along) + t, value)


def unpack_columns(read, store, sign, lane, nz):
    along, still, against = split_units(1, sign)
    for t, u in enumerate(along):
        store(u, read(t))
    base = len(along)
    for t, u in enumerate(still):
        store(u, read(base + t))
    half = LANES // 2
    for t, u in enumerate(against):
        first, second = read(base + 2 * t), read(base + 2 * t + 1)
        if sign > 0:
            value = jnp.where(lane < LANES - nz, pltpu.roll(first, half, 1), pltpu.roll(second, half + nz, 1))
        else:
            value = jnp.where(lane < nz, pltpu.roll(first, nz, 1), pltpu.roll(second, 2 * nz, 1))
        if u in wall_pair(1, sign):
            walls = read(base + 2 * len(against))
            if sign > 0:
                value = jnp.where(lane < half, pltpu.roll(walls, nz, 1), value)
            else:
                value = jnp.where(lane >= half, pltpu.roll(walls, LANES - nz, 1), value)
        store(u, value)


def relax(h, q, solid, inflow, emission, wind):
    w_rest, w_axis, w_diag = 1.0 / 3.0, 1.0 / 18.0, 1.0 / 36.0
    total = {k: h[k] + h[k + 1] for k in range(1, 19, 2)}
    gap = {k: h[k] - h[k + 1] for k in range(1, 19, 2)}
    xy, xz, yz = total[7] + total[9], total[11] + total[13], total[15] + total[17]
    axes = total[1] + total[3] + total[5]
    density = w_rest * h[0] + w_axis * axes + w_diag * (xy + xz + yz)
    ux = w_axis * gap[1] + w_diag * (gap[7] + gap[9] + gap[11] + gap[13])
    uy = w_axis * gap[3] + w_diag * (gap[7] - gap[9] + gap[15] + gap[17])
    uz = w_axis * gap[5] + w_diag * (gap[11] - gap[13] + gap[15] - gap[17])
    uxx, uyy, uzz = ux * ux, uy * uy, uz * uz
    third = w_rest * density
    pxx = w_axis * total[1] + w_diag * (xy + xz) - third - uxx
    pyy = w_axis * total[3] + w_diag * (xy + yz) - third - uyy
    pzz = w_axis * total[5] + w_diag * (xz + yz) - third - uzz
    pxy = w_diag * (total[7] - total[9]) - ux * uy
    pxz = w_diag * (total[11] - total[13]) - ux * uz
    pyz = w_diag * (total[15] - total[17]) - uy * uz
    cross = pxy * pxy + pxz * pxz + pyz * pyz
    contraction = pxx * pxx + pyy * pyy + pzz * pzz + (cross + cross)
    strength = 18.0 * math.sqrt(2.0) * SMAGORINSKY * SMAGORINSKY
    relax_time = 0.5 * (BASE_RELAX + jnp.sqrt(BASE_RELAX * BASE_RELAX + strength * jnp.sqrt(contraction)))
    rate = 1.0 / relax_time

    keep = 1.0 - 1.0 / TRACER_RELAX
    amount = 0.25 * q[0] + 0.125 * ((q[1] + q[2]) + (q[3] + q[4]) + (q[5] + q[6]))
    source = jnp.where(inflow, 0.0, amount * (1.0 / TRACER_RELAX))
    hold = jnp.where(inflow, 0.0, keep)
    level = source + jnp.where(inflow, 0.0, emission)
    push = 4.0 * source
    traced = [None] * 7
    traced[0] = jnp.where(solid, q[0], hold * q[0] + level)
    for k, speed in ((1, ux), (3, uy), (5, uz)):
        shift = push * speed
        traced[k] = jnp.where(solid, q[k + 1], hold * q[k] + (level + shift))
        traced[k + 1] = jnp.where(solid, q[k], hold * q[k + 1] + (level - shift))

    rate = jnp.where(inflow, 1.0, rate)
    density = jnp.where(inflow, 1.0, density)
    ux, uy, uz = (jnp.where(inflow, w, u) for w, u in zip(wind, (ux, uy, uz)))
    rest = 1.0 - rate
    square = ux * ux + uy * uy + uz * uz
    base = rate * (density - 1.5 * square)
    linear = 3.0 * rate
    quadratic = 4.5 * rate
    relaxed = [None] * 19
    relaxed[0] = jnp.where(solid, h[0], rest * h[0] + base)
    along = {1: ux, 3: uy, 5: uz, 7: ux + uy, 9: ux - uy, 11: ux + uz, 13: ux - uz, 15: uy + uz, 17: uy - uz}
    for k, speed in along.items():
        even = base + quadratic * speed * speed
        odd = linear * speed
        relaxed[k] = jnp.where(solid, h[k + 1], rest * h[k] + (even + odd))
        relaxed[k + 1] = jnp.where(solid, h[k], rest * h[k + 1] + (even - odd))
    return relaxed + traced


def lane_index():
    return lax.broadcasted_iota(jnp.int32, (ROWS, LANES), 1)


def wind_tiles(wind, nz):
    row = jnp.concatenate([wind[...]] * (LANES // nz), axis=1)
    return [jnp.broadcast_to(row[a : a + 1], (ROWS, LANES)) for a in range(3)]


def first_step(populations, tracer, solid, inflow, wind, emission, centre, y_up, y_down, x_up, x_down):
    extent = populations.shape[1]
    tiles = populations.shape[2] // LANES
    nz = wind.shape[1]
    winds = wind_tiles(wind, nz)
    lane = lane_index()
    height = lane % nz
    for j in range(tiles):
        lanes = slice(j * LANES, (j + 1) * LANES)
        for r in range(0, extent, ROWS):
            rows = slice(r, r + ROWS)
            h = [populations[k, rows, lanes] for k in range(FLOW)]
            q = [tracer[k, rows, lanes] for k in range(7)]
            built, held, emitted = solid[rows, lanes], inflow[rows, lanes], emission[rows, lanes]
            out = relax(h, q, built == 1, held == 1, emitted, winds)
            out += [built.astype(jnp.float32), held.astype(jnp.float32), emitted]
            for u in range(UNITS):
                centre[u, j, rows, :] = out[u]
        for sign, target, first in ((1, x_up, extent - STEPS), (-1, x_down, 0)):
            def store(offset, depth, value, target=target, j=j):
                target[j, offset : offset + depth, :] = value

            pack_rows(lambda u, low, depth, j=j: centre[u, j, low : low + depth, :], store, sign, first, height)
    for sign, target, j in ((1, y_up, tiles - 1), (-1, y_down, 0)):
        for r in range(0, extent, ROWS):
            rows = slice(r, r + ROWS)

            def store(t, value, target=target, rows=rows):
                target[t, rows, :] = value

            pack_columns(lambda u, j=j, rows=rows: centre[u, j, rows, :], store, sign, lane, nz)


def turn_corner(nz, from_south, from_north, sides, x_up, x_down):
    extent = sides.shape[2]
    lane = lane_index()
    height = lane % nz
    for side, (sign, source) in enumerate(((1, from_south), (-1, from_north))):
        for r in range(0, extent, ROWS):
            rows = slice(r, r + ROWS)

            def store(u, value, side=side, rows=rows):
                sides[u, side, rows, :] = value

            unpack_columns(lambda t, source=source, rows=rows: source[t, rows, :], store, sign, lane, nz)
        for sign_x, target, first in ((1, x_up, extent - STEPS), (-1, x_down, 0)):
            def put(offset, depth, value, target=target, side=side):
                target[side, offset : offset + depth, :] = value

            pack_rows(lambda u, low, depth, side=side: sides[u, side, low : low + depth, :], put, sign_x, first, height)


def later_steps(centre, sides, wind, west, east, corner_west, corner_east, flow_out, tracer_out, grown, ping, pong):
    tiles, extent = centre.shape[1], centre.shape[2]
    wide = tiles + 2
    nz = wind.shape[1]
    winds = wind_tiles(wind, nz)
    lane = lane_index()
    height = lane % nz
    for u in range(UNITS):
        for j in range(wide):
            for r in range(0, extent, ROWS):
                if j == 0:
                    value = sides[u, 0, r : r + ROWS, :]
                elif j == wide - 1:
                    value = sides[u, 1, r : r + ROWS, :]
                else:
                    value = centre[u, j - 1, r : r + ROWS, :]
                grown[u, j, STEPS + r : STEPS + r + ROWS, :] = value
    for j in range(wide):
        inner = 1 <= j <= tiles
        at = j - 1 if inner else (0 if j == 0 else 1)
        for sign, source, first in (
            (1, west if inner else corner_west, 0),
            (-1, east if inner else corner_east, STEPS + extent),
        ):

            def fill(u, row, value, j=j):
                grown[u, j, row : row + value.shape[0], :] = value

            unpack_rows(
                lambda offset, depth, source=source, at=at: source[at, offset : offset + depth, :], fill, sign, first
            )

    def pulled(buffer, u, j, before, after, r):
        step_x, step_y, step_z = SPEED[u]
        rows = pl.ds(r - step_x, ROWS)
        value = buffer[u, j, rows, :]
        if step_y == 1:
            value = jnp.where(lane >= LANES - nz, buffer[u, before, rows, :], value)
        elif step_y == -1:
            value = jnp.where(lane < nz, buffer[u, after, rows, :], value)
        shift = (nz * step_y + step_z) % LANES
        if shift:
            value = pltpu.roll(value, shift, 1)
        if step_z:
            edge = height == (0 if step_z == 1 else nz - 1)
            value = jnp.where(edge, buffer[TURNED[u], j, pl.ds(r, ROWS), :], value)
        return value

    source = grown
    for step in range(1, STEPS):
        target = ping if step % 2 else pong
        low, high = step, extent + 2 * STEPS - step
        firsts = list(range(low, high - ROWS, ROWS)) + [high - ROWS]

        def column(j, _, source=source, target=target, firsts=firsts):
            before, after = jnp.maximum(j - 1, 0), jnp.minimum(j + 1, wide - 1)
            for r in firsts:
                moved = [pulled(source, u, j, before, after, r) for u in range(MOVING)]
                cells = pl.ds(r, ROWS)
                out = relax(
                    moved[:FLOW],
                    moved[FLOW:],
                    grown[SOLID, j, cells, :] == 1.0,
                    grown[INFLOW, j, cells, :] == 1.0,
                    grown[EMISSION, j, cells, :],
                    winds,
                )
                for u in range(MOVING):
                    target[u, j, cells, :] = out[u]
            return _

        lax.fori_loop(0, wide, column, 0)
        source = target
    for j in range(1, tiles + 1):
        lanes = slice((j - 1) * LANES, j * LANES)
        for r in range(0, extent, ROWS):
            for u in range(MOVING):
                value = pulled(source, u, j, j - 1, j + 1, STEPS + r)
                if u < FLOW:
                    flow_out[u, r : r + ROWS, lanes] = value
                else:
                    tracer_out[u - FLOW, r : r + ROWS, lanes] = value


def passed_along(shard, axis, by):
    length = lax.axis_size(axis)
    return lax.ppermute(shard, axis, [(i, (i + by) % length) for i in range(length)])


def near(x):
    return pltpu.with_memory_space_constraint(x, pltpu.VMEM)


def local(populations, tracer, solid_mask, inflow, wind_profile, emission):
    extent = populations.shape[1]
    tiles = populations.shape[2] // LANES
    nz = wind_profile.shape[1]
    along, still, _ = split_units(1, 1)
    messages = len(along) + len(still)
    packed = row_plan(1)[2]
    vm = lambda *shape: pltpu.VMEM(shape, jnp.float32)
    plain = lambda *shape: jax.ShapeDtypeStruct(shape, jnp.float32)
    centre, y_up, y_down, x_up, x_down = pl.pallas_call(
        first_step,
        out_shape=(
            vm(UNITS, tiles, extent, LANES),
            vm(messages, extent, LANES),
            vm(messages, extent, LANES),
            vm(tiles, packed, LANES),
            vm(tiles, packed, LANES),
        ),
        name="first_step",
    )(populations, tracer, solid_mask, inflow, wind_profile, emission)
    from_south = passed_along(y_up, "gy", 1)
    from_north = passed_along(y_down, "gy", -1)
    west = passed_along(x_up, "gx", 1)
    east = passed_along(x_down, "gx", -1)
    sides, corner_up, corner_down = pl.pallas_call(
        lambda *refs: turn_corner(nz, *refs),
        out_shape=(vm(UNITS, 2, extent, LANES), vm(2, packed, LANES), vm(2, packed, LANES)),
        name="turn_corner",
    )(near(from_south), near(from_north))
    corner_west = passed_along(corner_up, "gx", 1)
    corner_east = passed_along(corner_down, "gx", -1)
    rows = extent + 2 * STEPS
    return pl.pallas_call(
        later_steps,
        out_shape=(plain(FLOW, extent, tiles * LANES), plain(7, extent, tiles * LANES)),
        scratch_shapes=[
            vm(UNITS, tiles + 2, rows, LANES),
            vm(MOVING, tiles + 2, rows, LANES),
            vm(MOVING, tiles + 2, rows, LANES),
        ],
        name="later_steps",
    )(near(centre), near(sides), wind_profile, near(west), near(east), near(corner_west), near(corner_east))


def solution(mesh):
    in_specs = (
        P(None, "gx", "gy"),
        P(None, "gx", "gy"),
        P("gx", "gy"),
        P("gx", "gy"),
        P(),
        P("gx", "gy"),
    )
    out_specs = (P(None, "gx", "gy"), P(None, "gx", "gy"))
    return jax.shard_map(local, mesh=mesh, in_specs=in_specs, out_specs=out_specs, check_vma=False)
```

time: 60.2 us -> 27.2 us (0.45)
  the two profiles are of different devices: /device:TPU:0 before, /device:TPU:1 now
where the time goes in v1:
time: 27.2 us; the launch traced here: 27 us
  starting transfers between devices  10.3 us (38%)
  waiting for transfers between devices  8.06 us (30%)
  Pallas kernels  7.95 us (29%)
  between operations  0.65 us (2%)
    ppermute x6, starting transfers between devices, passed_along(): lax.ppermute(shard, axis, [(i, (i + by) % length) for i in range(length)])  10.3 us
    ppermute x6, waiting for transfers between devices, passed_along(): lax.ppermute(shard, axis, [(i, (i + by) % length) for i in range(length)])  8.06 us
    pallas_call x1, Pallas kernels, local(): pl.pallas_call(later_steps, out_shape=(plain(FLOW, extent, tiles * LANES)...  6.04 us
    pallas_call x1, Pallas kernels, local(): pl.pallas_call(first_step, out_shape=(vm(UNITS, tiles, extent, LANES), vm...  1.75 us
  transfers between devices with their start and end apart: 6, of which 4 were waited for; matrix products, arithmetic and copies ran while one was open for 0% of the time, Pallas kernels for 1%

profile of v1, /device:TPU:1, one launch (start us, length us, event | category | flops | bytes accessed | tf_op | source)
XLA Modules:
  0.0 27.0 jit_solution(9384219524285916427)
XLA Ops:
  0.6 1.7 %first_step.1 = (f32[29,4,16,128]{3,2,1,0:T(8,128)S(1)}, f32[23,16,128]{2,1,0:T(8,128)S(1)}, f32[23,16,128]{2,1,0:T(8,128)S(1)}, f32[4,88,128]{2,1,0:T(8,128)S(1)}, f32[4,88,128]{2,1,0:T(8,128)S(1)}) custom-call(f32[19,16,512]{2,1,0:T(8,128)} %populations.1, f32[7,16,512]{2,1,0:T(8,128)} %tracer.1, s32[16,512]{1,0:T(8,128)} %solid.1, s32[16,512]{1,0:T(8,128)} %inflow.1, ...), custom_call_target="tpu_custom_call" | custom-call | tf_op jit(solution)/shard_map/first_step/pallas_call | solution.py:351
  2.4 2.1 %collective-permute-start = (f32[23,16,128]{2,1,0:T(8,128)S(1)}, f32[23,16,128]{2,1,0:T(8,128)S(1)}, u32[]{:S(2)}, u32[]{:S(2)}) collective-permute-start(f32[23,16,128]{2,1,0:T(8,128)S(1)} %get-tuple-element.11), channel_id=1, source_target_pairs={{0,1},{1,2},{2,3},{3,4},{4,5},{5,6},{6,7},{7,0},{8,9},{9,10},{10,1... | collective-permute-start | bytes 565256 | tf_op jit(solution)/shard_map/ppermute | solution.py:335
  4.5 3.1 %collective-permute-start.1 = (f32[23,16,128]{2,1,0:T(8,128)S(1)}, f32[23,16,128]{2,1,0:T(8,128)S(1)}, u32[]{:S(2)}, u32[]{:S(2)}) collective-permute-start(f32[23,16,128]{2,1,0:T(8,128)S(1)} %get-tuple-element.12), channel_id=1, source_target_pairs={{0,7},{1,0},{2,1},{3,2},{4,3},{5,4},{6,5},{7,6},{8,15},{9,8},{10,9... | collective-permute-start | bytes 565256 | tf_op jit(solution)/shard_map/ppermute | solution.py:335
  7.6 2.2 %collective-permute-start.2 = (f32[4,88,128]{2,1,0:T(8,128)S(1)}, f32[4,88,128]{2,1,0:T(8,128)S(1)}, u32[]{:S(2)}, u32[]{:S(2)}) collective-permute-start(f32[4,88,128]{2,1,0:T(8,128)S(1)} %get-tuple-element.14), channel_id=1, source_target_pairs={{0,8},{8,16},{16,24},{24,0},{1,9},{9,17},{17,25},{25,1},{2,10},{10... | collective-permute-start | bytes 540680 | tf_op jit(solution)/shard_map/ppermute | solution.py:335
  9.8 0.0 collective-permute-start.3
  9.8 2.2 %collective-permute-done.refs_0_ = f32[23,16,128]{2,1,0:T(8,128)S(1)} collective-permute-done((f32[23,16,128]{2,1,0:T(8,128)S(1)}, f32[23,16,128]{2,1,0:T(8,128)S(1)}, u32[]{:S(2)}, u32[]{:S(2)}) %collective-permute-start) | collective-permute-done | bytes 188448 | tf_op jit(solution)/shard_map/ppermute | solution.py:335
  12.0 1.9 %collective-permute-done.1.refs_1_ = f32[23,16,128]{2,1,0:T(8,128)S(1)} collective-permute-done((f32[23,16,128]{2,1,0:T(8,128)S(1)}, f32[23,16,128]{2,1,0:T(8,128)S(1)}, u32[]{:S(2)}, u32[]{:S(2)}) %collective-permute-start.1) | collective-permute-done | bytes 188448 | tf_op jit(solution)/shard_map/ppermute | solution.py:335
  13.9 0.2 turn_corner.1
  14.0 3.0 %collective-permute-start.4 = (f32[2,88,128]{2,1,0:T(8,128)S(1)}, f32[2,88,128]{2,1,0:T(8,128)S(1)}, u32[]{:S(2)}, u32[]{:S(2)}) collective-permute-start(f32[2,88,128]{2,1,0:T(8,128)S(1)} %get-tuple-element.16), channel_id=1, source_target_pairs={{0,8},{8,16},{16,24},{24,0},{1,9},{9,17},{17,25},{25,1},{2,10},{10... | collective-permute-start | bytes 270344 | tf_op jit(solution)/shard_map/ppermute | solution.py:335
  17.0 0.0 collective-permute-start.5
  17.0 0.0 collective-permute-done.2.west
  17.0 0.0 collective-permute-done.3.east
  17.0 1.6 %collective-permute-done.4.corner_west = f32[2,88,128]{2,1,0:T(8,128)S(1)} collective-permute-done((f32[2,88,128]{2,1,0:T(8,128)S(1)}, f32[2,88,128]{2,1,0:T(8,128)S(1)}, u32[]{:S(2)}, u32[]{:S(2)}) %collective-permute-start.4) | collective-permute-done | bytes 90144 | tf_op jit(solution)/shard_map/ppermute | solution.py:335
  18.6 2.4 %collective-permute-done.5.corner_east = f32[2,88,128]{2,1,0:T(8,128)S(1)} collective-permute-done((f32[2,88,128]{2,1,0:T(8,128)S(1)}, f32[2,88,128]{2,1,0:T(8,128)S(1)}, u32[]{:S(2)}, u32[]{:S(2)}) %collective-permute-start.5) | collective-permute-done | bytes 90144 | tf_op jit(solution)/shard_map/ppermute | solution.py:335
  20.9 6.0 %later_steps.1 = (f32[19,16,512]{2,1,0:T(8,128)}, f32[7,16,512]{2,1,0:T(8,128)}) custom-call(f32[29,4,16,128]{3,2,1,0:T(8,128)S(1)} %get-tuple-element.10.centre, f32[29,2,16,128]{3,2,1,0:T(8,128)S(1)} %get-tuple-element.13.sides, f32[3,32]{1,0:T(4,128)} %wind.3, f32[4,88,128]{2,1,0:T(8,128)S(1)} %collective-permute-done.2.west, ...), custom_call_target="tpu_custom_call" | custom-call | tf_op jit(solution)/shard_map/later_steps/pallas_call | solution.py:374
Async XLA Ops:
  2.4 9.6 %collective-permute-start = (f32[23,16,128]{2,1,0:T(8,128)S(1)}, f32[23,16,128]{2,1,0:T(8,128)S(1)}, u32[]{:S(2)}, u32[]{:S(2)}) collective-permute-start(f32[23,16,128]{2,1,0:T(8,128)S(1)} %get-tuple-element.11), channel_id=1, source_target_pairs={{0,1},{1,2},{2,3},{3,4},{4,5},{5,6},{6,7},{7,0},{8,9},{9,10},{10,1... | collective-permute-start | bytes 565256 | tf_op jit(solution)/shard_map/ppermute | solution.py:335
  4.5 9.4 %collective-permute-start.1 = (f32[23,16,128]{2,1,0:T(8,128)S(1)}, f32[23,16,128]{2,1,0:T(8,128)S(1)}, u32[]{:S(2)}, u32[]{:S(2)}) collective-permute-start(f32[23,16,128]{2,1,0:T(8,128)S(1)} %get-tuple-element.12), channel_id=1, source_target_pairs={{0,7},{1,0},{2,1},{3,2},{4,3},{5,4},{6,5},{7,6},{8,15},{9,8},{10,9... | collective-permute-start | bytes 565256 | tf_op jit(solution)/shard_map/ppermute | solution.py:335
  7.6 9.4 %collective-permute-start.2 = (f32[4,88,128]{2,1,0:T(8,128)S(1)}, f32[4,88,128]{2,1,0:T(8,128)S(1)}, u32[]{:S(2)}, u32[]{:S(2)}) collective-permute-start(f32[4,88,128]{2,1,0:T(8,128)S(1)} %get-tuple-element.14), channel_id=1, source_target_pairs={{0,8},{8,16},{16,24},{24,0},{1,9},{9,17},{17,25},{25,1},{2,10},{10... | collective-permute-start | bytes 540680 | tf_op jit(solution)/shard_map/ppermute | solution.py:335
  9.8 7.2 %collective-permute-start.3 = (f32[4,88,128]{2,1,0:T(8,128)S(1)}, f32[4,88,128]{2,1,0:T(8,128)S(1)}, u32[]{:S(2)}, u32[]{:S(2)}) collective-permute-start(f32[4,88,128]{2,1,0:T(8,128)S(1)} %get-tuple-element.15), channel_id=1, source_target_pairs={{0,24},{8,0},{16,8},{24,16},{1,25},{9,1},{17,9},{25,17},{2,26},{10... | collective-permute-start | bytes 540680 | tf_op jit(solution)/shard_map/ppermute | solution.py:335
  14.0 4.5 %collective-permute-start.4 = (f32[2,88,128]{2,1,0:T(8,128)S(1)}, f32[2,88,128]{2,1,0:T(8,128)S(1)}, u32[]{:S(2)}, u32[]{:S(2)}) collective-permute-start(f32[2,88,128]{2,1,0:T(8,128)S(1)} %get-tuple-element.16), channel_id=1, source_target_pairs={{0,8},{8,16},{16,24},{24,0},{1,9},{9,17},{17,25},{25,1},{2,10},{10... | collective-permute-start | bytes 270344 | tf_op jit(solution)/shard_map/ppermute | solution.py:335
  17.0 4.0 %collective-permute-start.5 = (f32[2,88,128]{2,1,0:T(8,128)S(1)}, f32[2,88,128]{2,1,0:T(8,128)S(1)}, u32[]{:S(2)}, u32[]{:S(2)}) collective-permute-start(f32[2,88,128]{2,1,0:T(8,128)S(1)} %get-tuple-element.17), channel_id=1, source_target_pairs={{0,24},{8,0},{16,8},{24,16},{1,25},{9,1},{17,9},{25,17},{2,26},{10... | collective-permute-start | bytes 270344 | tf_op jit(solution)/shard_map/ppermute | solution.py:335

commit v2 on v1

--- a/solution.py
+++ b/solution.py
@@ -7,8 +7,10 @@
 from jax.experimental.pallas import tpu as pltpu
 from jax.sharding import PartitionSpec as P
 
+
 STEPS = 4
 LANES = 128
+KERNEL_BYTES = 16 * 2**20
 ROWS = 8
 
 LATTICE = (
@@ -189,45 +191,111 @@
     return lax.broadcasted_iota(jnp.int32, (ROWS, LANES), 1)
 
 
-def wind_tiles(wind, nz):
-    row = jnp.concatenate([wind[...]] * (LANES // nz), axis=1)
-    return [jnp.broadcast_to(row[a : a + 1], (ROWS, LANES)) for a in range(3)]
-
-
-def first_step(populations, tracer, solid, inflow, wind, emission, centre, y_up, y_down, x_up, x_down):
+def wind_tiles(wind):
+    return [jnp.broadcast_to(wind[a : a + 1, :], (ROWS, LANES)) for a in range(3)]
+
+
+def start_all(copies, sems):
+    started = [pltpu.make_async_copy(src, dst, sems.at[n]) for n, (src, dst) in enumerate(copies)]
+    for copy in started:
+        copy.start()
+    return started
+
+
+def relax_own(cells, winds, store, rows):
+    populations, tracer, solid, inflow, emission = cells
+    h = [populations[k, rows, :] for k in range(FLOW)]
+    q = [tracer[k, rows, :] for k in range(7)]
+    built, held, emitted = solid[rows, :], inflow[rows, :], emission[rows, :]
+    out = relax(h, q, built == 1, held == 1, emitted, winds)
+    for u, value in enumerate(out + [built.astype(jnp.float32), held.astype(jnp.float32), emitted]):
+        store(u, value)
+
+
+def load_tiles(arrays, buffers, columns, sems, extra=()):
+    copies = list(extra)
+    for n, j in enumerate(columns):
+        lanes = pl.ds(j * LANES, LANES)
+        for array, buffer in zip(arrays, buffers):
+            src = array.at[:, :, lanes] if len(array.shape) == 3 else array.at[:, lanes]
+            copies.append((src, buffer.at[n]))
+    started = start_all(copies, sems)
+    count = len(arrays)
+    own = [started[len(extra) + n * count : len(extra) + (n + 1) * count] for n in range(len(columns))]
+    return started[: len(extra)], own
+
+
+def first_edges(
+    populations, tracer, solid, inflow, wind, emission, edge, winds, y_up, y_down,
+    wind_in, pop_in, tracer_in, solid_in, inflow_in, emission_in, sems,
+):
     extent = populations.shape[1]
     tiles = populations.shape[2] // LANES
     nz = wind.shape[1]
-    winds = wind_tiles(wind, nz)
     lane = lane_index()
-    height = lane % nz
-    for j in range(tiles):
-        lanes = slice(j * LANES, (j + 1) * LANES)
+    buffers = (pop_in, tracer_in, solid_in, inflow_in, emission_in)
+    common, own = load_tiles(
+        (populations, tracer, solid, inflow, emission), buffers, (tiles - 1, 0), sems, ((wind, wind_in),)
+    )
+    for copy in common:
+        copy.wait()
+    winds[...] = jnp.concatenate([wind_in[...]] * (LANES // nz), axis=1)
+    wind_values = wind_tiles(winds)
+    for n, (at, sign, target) in enumerate(((1, 1, y_up), (0, -1, y_down))):
+        for copy in own[n]:
+            copy.wait()
+        cells = [b.at[n] for b in buffers]
         for r in range(0, extent, ROWS):
             rows = slice(r, r + ROWS)
-            h = [populations[k, rows, lanes] for k in range(FLOW)]
-            q = [tracer[k, rows, lanes] for k in range(7)]
-            built, held, emitted = solid[rows, lanes], inflow[rows, lanes], emission[rows, lanes]
-            out = relax(h, q, built == 1, held == 1, emitted, winds)
-            out += [built.astype(jnp.float32), held.astype(jnp.float32), emitted]
-            for u in range(UNITS):
-                centre[u, j, rows, :] = out[u]
-        for sign, target, first in ((1, x_up, extent - STEPS), (-1, x_down, 0)):
-            def store(offset, depth, value, target=target, j=j):
-                target[j, offset : offset + depth, :] = value
-
-            pack_rows(lambda u, low, depth, j=j: centre[u, j, low : low + depth, :], store, sign, first, height)
-    for sign, target, j in ((1, y_up, tiles - 1), (-1, y_down, 0)):
+
+            def keep(u, value, at=at, rows=rows):
+                edge[u, at, rows, :] = value
+
+            relax_own(cells, wind_values, keep, rows)
         for r in range(0, extent, ROWS):
             rows = slice(r, r + ROWS)
 
-            def store(t, value, target=target, rows=rows):
+            def send(t, value, target=target, rows=rows):
                 target[t, rows, :] = value
 
-            pack_columns(lambda u, j=j, rows=rows: centre[u, j, rows, :], store, sign, lane, nz)
-
-
-def turn_corner(nz, from_south, from_north, sides, x_up, x_down):
+            pack_columns(lambda u, at=at, rows=rows: edge[u, at, rows, :], send, sign, lane, nz)
+
+
+def first_inner(
+    populations, tracer, solid, inflow, emission, winds, edge, inner, x_up, x_down,
+    pop_in, tracer_in, solid_in, inflow_in, emission_in, sems, *, nz,
+):
+    extent = populations.shape[1]
+    tiles = populations.shape[2] // LANES
+    height = lane_index() % nz
+    buffers = (pop_in, tracer_in, solid_in, inflow_in, emission_in)
+    columns = tuple(range(1, tiles - 1))
+    _, own = load_tiles((populations, tracer, solid, inflow, emission), buffers, columns, sems)
+    wind_values = wind_tiles(winds)
+
+    def pack(j, source, at):
+        for sign, target, first in ((1, x_up, extent - STEPS), (-1, x_down, 0)):
+            def store(offset, depth, value, target=target):
+                target[j, offset : offset + depth, :] = value
+
+            pack_rows(lambda u, low, depth: source[u, at, low : low + depth, :], store, sign, first, height)
+
+    pack(0, edge, 0)
+    pack(tiles - 1, edge, 1)
+    for n, j in enumerate(columns):
+        for copy in own[n]:
+            copy.wait()
+        for r in range(0, extent, ROWS):
+            rows = slice(r, r + ROWS)
+
+            def keep(u, value, n=n, rows=rows):
+                inner[u, n, rows, :] = value
+
+            relax_own([b.at[n] for b in buffers], wind_values, keep, rows)
+        pack(j, inner, n)
+
+
+def turn_corner(from_south, from_north, sides, x_up, x_down, *, nz):
     extent = sides.shape[2]
     lane = lane_index()
     height = lane % nz
@@ -246,141 +314,286 @@
             pack_rows(lambda u, low, depth, side=side: sides[u, side, low : low + depth, :], put, sign_x, first, height)
 
 
-def later_steps(centre, sides, wind, west, east, corner_west, corner_east, flow_out, tracer_out, grown, ping, pong):
-    tiles, extent = centre.shape[1], centre.shape[2]
-    wide = tiles + 2
-    nz = wind.shape[1]
-    winds = wind_tiles(wind, nz)
-    lane = lane_index()
-    height = lane % nz
-    for u in range(UNITS):
-        for j in range(wide):
-            for r in range(0, extent, ROWS):
-                if j == 0:
-                    value = sides[u, 0, r : r + ROWS, :]
-                elif j == wide - 1:
-                    value = sides[u, 1, r : r + ROWS, :]
-                else:
-                    value = centre[u, j - 1, r : r + ROWS, :]
-                grown[u, j, STEPS + r : STEPS + r + ROWS, :] = value
-    for j in range(wide):
-        inner = 1 <= j <= tiles
-        at = j - 1 if inner else (0 if j == 0 else 1)
-        for sign, source, first in (
-            (1, west if inner else corner_west, 0),
-            (-1, east if inner else corner_east, STEPS + extent),
-        ):
-
-            def fill(u, row, value, j=j):
-                grown[u, j, row : row + value.shape[0], :] = value
-
-            unpack_rows(
-                lambda offset, depth, source=source, at=at: source[at, offset : offset + depth, :], fill, sign, first
-            )
-
-    def pulled(buffer, u, j, before, after, r):
+class Mover:
+    def __init__(self, nz):
+        lane = lane_index()
+        height = lane % nz
+        self.nz = nz
+        self.from_part = [None] + [lane >= part * nz for part in range(1, LANES // nz)]
+        self.floor, self.roof = height == 0, height == nz - 1
+
+    def merge(self, read, columns):
+        value = read(columns[0])
+        for part in range(1, len(columns)):
+            if columns[part] != columns[part - 1]:
+                value = jnp.where(self.from_part[part], read(columns[part]), value)
+        return value
+
+    def pull(self, read, parts, u, r):
         step_x, step_y, step_z = SPEED[u]
-        rows = pl.ds(r - step_x, ROWS)
-        value = buffer[u, j, rows, :]
-        if step_y == 1:
-            value = jnp.where(lane >= LANES - nz, buffer[u, before, rows, :], value)
-        elif step_y == -1:
-            value = jnp.where(lane < nz, buffer[u, after, rows, :], value)
-        shift = (nz * step_y + step_z) % LANES
+        value = self.merge(lambda c: read(u, c, r - step_x), parts[step_y])
+        shift = (self.nz * step_y + step_z) % LANES
         if shift:
             value = pltpu.roll(value, shift, 1)
         if step_z:
-            edge = height == (0 if step_z == 1 else nz - 1)
-            value = jnp.where(edge, buffer[TURNED[u], j, pl.ds(r, ROWS), :], value)
+            own = self.merge(lambda c: read(TURNED[u], c, r), parts[0])
+            value = jnp.where(self.floor if step_z == 1 else self.roof, own, value)
         return value
 
-    source = grown
+
+def plain_parts(column, before, after, count):
+    return {0: [column] * count, 1: [column] * (count - 1) + [before], -1: [after] + [column] * (count - 1)}
+
+
+def row_starts(step, rows):
+    low, high = step, rows - step
+    return list(range(low, high - ROWS, ROWS)) + [high - ROWS]
+
+
+def relax_column(mover, read, fields, parts, here, step, rows, winds, store):
+    for r in row_starts(step, rows):
+        moved = [mover.pull(read, parts, u, r) for u in range(MOVING)]
+        solid, inflow, emission = (mover.merge(lambda c, u=u: fields(u, c, r), here) for u in (SOLID, INFLOW, EMISSION))
+        out = relax(moved[:FLOW], moved[FLOW:], solid == 1.0, inflow == 1.0, emission, winds)
+        for u in range(MOVING):
+            store(u, r, out[u])
+
+
+def inner_steps(edge, inner, winds, west, east, one, two, three, four, done, *, nz):
+    tiles, rows = one.shape[1], one.shape[2]
+    extent = rows - 2 * STEPS
+    count = LANES // nz
+    mover = Mover(nz)
+    wind_values = wind_tiles(winds)
+    for j in range(tiles):
+        for u in range(UNITS):
+            for r in range(0, extent, ROWS):
+                cells = slice(r, r + ROWS)
+                if j in (0, tiles - 1):
+                    value = edge[u, 0 if j == 0 else 1, cells, :]
+                else:
+                    value = inner[u, j - 1, cells, :]
+                one[u, j, STEPS + r : STEPS + r + ROWS, :] = value
+        for sign, source, first in ((1, west, 0), (-1, east, STEPS + extent)):
+            def fill(u, row, value, j=j):
+                one[u, j, row : row + value.shape[0], :] = value
+
+            unpack_rows(
+                lambda offset, depth, source=source, j=j: source[j, offset : offset + depth, :], fill, sign, first
+            )
+    levels = (one, two, three, four)
     for step in range(1, STEPS):
-        target = ping if step % 2 else pong
-        low, high = step, extent + 2 * STEPS - step
-        firsts = list(range(low, high - ROWS, ROWS)) + [high - ROWS]
-
-        def column(j, _, source=source, target=target, firsts=firsts):
-            before, after = jnp.maximum(j - 1, 0), jnp.minimum(j + 1, wide - 1)
-            for r in firsts:
-                moved = [pulled(source, u, j, before, after, r) for u in range(MOVING)]
-                cells = pl.ds(r, ROWS)
-                out = relax(
-                    moved[:FLOW],
-                    moved[FLOW:],
-                    grown[SOLID, j, cells, :] == 1.0,
-                    grown[INFLOW, j, cells, :] == 1.0,
-                    grown[EMISSION, j, cells, :],
-                    winds,
-                )
-                for u in range(MOVING):
-                    target[u, j, cells, :] = out[u]
-            return _
-
-        lax.fori_loop(0, wide, column, 0)
-        source = target
-    for j in range(1, tiles + 1):
-        lanes = slice((j - 1) * LANES, j * LANES)
+        source, target = levels[step - 1], levels[step]
+
+        def column(j, carry, source=source, target=target, step=step):
+            before, after = jnp.maximum(j - 1, 0), jnp.minimum(j + 1, tiles - 1)
+            names = {"here": j, "before": before, "after": after}
+
+            def store(u, r, value):
+                target[u, j, pl.ds(r, ROWS), :] = value
+
+            relax_column(
+                mover,
+                lambda u, c, r: source[u, names[c], pl.ds(r, ROWS), :],
+                lambda u, c, r: one[u, names[c], pl.ds(r, ROWS), :],
+                plain_parts("here", "before", "after", count),
+                ["here"] * count,
+                step,
+                rows,
+                wind_values,
+                store,
+            )
+            return carry
+
+        lax.fori_loop(0, tiles, column, 0)
+    for j in range(1, tiles - 1):
         for r in range(0, extent, ROWS):
             for u in range(MOVING):
-                value = pulled(source, u, j, j - 1, j + 1, STEPS + r)
-                if u < FLOW:
-                    flow_out[u, r : r + ROWS, lanes] = value
-                else:
-                    tracer_out[u - FLOW, r : r + ROWS, lanes] = value
+                done[u, j - 1, r : r + ROWS, :] = mover.pull(
+                    lambda u, c, at: four[u, c, at : at + ROWS, :], plain_parts(j, j - 1, j + 1, count), u, STEPS + r
+                )
+
+
+def outer_steps(
+    one, two, three, four, done, winds, sides, corner_west, corner_east, flow_out, tracer_out,
+    margin, outer_two, outer_three, outer_four, edge_done, sems, *, nz,
+):
+    tiles, rows = one.shape[1], one.shape[2]
+    extent = rows - 2 * STEPS
+    count = LANES // nz
+    part = count // 2
+    mover = Mover(nz)
+    wind_values = wind_tiles(winds)
+    last = tiles + 1
+    copies = []
+
+    def write_out(source, at, j):
+        lanes = pl.ds(j * LANES, LANES)
+        for units, target in (((0, FLOW), flow_out), ((FLOW, MOVING), tracer_out)):
+            copy = pltpu.make_async_copy(
+                source.at[pl.ds(units[0], units[1] - units[0]), at], target.at[:, :, lanes], sems.at[len(copies)]
+            )
+            copy.start()
+            copies.append(copy)
+
+    for j in range(1, tiles - 1):
+        write_out(done, j - 1, j)
+    for side in range(2):
+        for u in range(UNITS):
+            for r in range(0, extent, ROWS):
+                margin[u, side, STEPS + r : STEPS + r + ROWS, :] = sides[u, side, r : r + ROWS, :]
+        for sign_x, corner, first in ((1, corner_west, 0), (-1, corner_east, STEPS + extent)):
+            def fill(u, row, value, side=side):
+                margin[u, side, row : row + value.shape[0], :] = value
+
+            unpack_rows(
+                lambda offset, depth, corner=corner, side=side: corner[side, offset : offset + depth, :],
+                fill,
+                sign_x,
+                first,
+            )
+
+    both = -1
+    outer = (
+        None,
+        {0: (margin, 0), last: (margin, 1)},
+        {0: (outer_two, 0), 1: (outer_two, 1), tiles: (outer_two, 2), last: (outer_two, 3)},
+        {both: (outer_three, 2), 1: (outer_three, 0), tiles: (outer_three, 1)},
+        {both: (outer_four, 2), 1: (outer_four, 0), tiles: (outer_four, 1)},
+    )
+    own = (None, one, two, three, four)
+
+    def reader(level):
+        def read(u, c, r):
+            ref, at = outer[level].get(c, (own[level], c - 1))
+            return ref[u, at, r : r + ROWS, :]
+
+        return read
+
+    def parts_of(level, c):
+        if c == both and level == 2:
+            return {
+                0: [last] * part + [0] * (count - part),
+                1: [last] * (part - 1) + [0] * (count - part) + [tiles],
+                -1: [1] + [last] * part + [0] * (count - part - 1),
+            }
+        if c == both:
+            return plain_parts(both, tiles, 1, count)
+        before = both if c == 1 and level > 2 else max(c - 1, 0)
+        after = both if c == tiles and level > 2 else min(c + 1, last)
+        return plain_parts(c, before, after, count)
+
+    for step in range(1, STEPS):
+        for c, (target, at) in outer[step + 1].items():
+            def store(u, r, value, target=target, at=at):
+                target[u, at, r : r + ROWS, :] = value
+
+            parts = parts_of(step, c)
+            here = parts if c != both else parts_of(2, both)
+            relax_column(mover, reader(step), reader(1), parts, here[0], step, rows, wind_values, store)
+    for n, c in enumerate((1, tiles)):
+        for r in range(0, extent, ROWS):
+            for u in range(MOVING):
+                edge_done[u, n, r : r + ROWS, :] = mover.pull(reader(STEPS), parts_of(STEPS, c), u, STEPS + r)
+        write_out(edge_done, n, c - 1)
+    for copy in copies:
+        copy.wait()
 
 
 def passed_along(shard, axis, by):
     length = lax.axis_size(axis)
     return lax.ppermute(shard, axis, [(i, (i + by) % length) for i in range(length)])
-
-
-def near(x):
-    return pltpu.with_memory_space_constraint(x, pltpu.VMEM)
 
 
 def local(populations, tracer, solid_mask, inflow, wind_profile, emission):
     extent = populations.shape[1]
     tiles = populations.shape[2] // LANES
     nz = wind_profile.shape[1]
+    inner_tiles = tiles - 2
     along, still, _ = split_units(1, 1)
     messages = len(along) + len(still)
     packed = row_plan(1)[2]
+    rows = extent + 2 * STEPS
     vm = lambda *shape: pltpu.VMEM(shape, jnp.float32)
-    plain = lambda *shape: jax.ShapeDtypeStruct(shape, jnp.float32)
-    centre, y_up, y_down, x_up, x_down = pl.pallas_call(
-        first_step,
-        out_shape=(
-            vm(UNITS, tiles, extent, LANES),
+    far = pl.BlockSpec(memory_space=pltpu.HBM)
+    close = pl.BlockSpec(memory_space=pltpu.VMEM)
+
+    def buffers(number):
+        return [
+            vm(number, FLOW, extent, LANES),
+            vm(number, 7, extent, LANES),
+            pltpu.VMEM((number, extent, LANES), jnp.int32),
+            pltpu.VMEM((number, extent, LANES), jnp.int32),
+            vm(number, extent, LANES),
+            pltpu.SemaphoreType.DMA((5 * number + 1,)),
+        ]
+
+    def run(body, out_shape, args, far_args=0, out_specs=None, scratch=()):
+        specs = [far] * far_args + [close] * (len(args) - far_args)
+        args = tuple(pltpu.with_memory_space_constraint(a, pltpu.HBM if n < far_args else pltpu.VMEM) for n, a in enumerate(args))
+        options = {} if out_specs is None else {"out_specs": out_specs}
+        return pl.pallas_call(
+            body,
+            out_shape=out_shape,
+            in_specs=specs,
+            scratch_shapes=list(scratch),
+            compiler_params=pltpu.CompilerParams(vmem_limit_bytes=KERNEL_BYTES),
+            **options,
+        )(*args)
+
+    edge, winds, y_up, y_down = run(
+        first_edges,
+        (
+            vm(UNITS, 2, extent, LANES),
+            vm(3, LANES),
             vm(messages, extent, LANES),
             vm(messages, extent, LANES),
-            vm(tiles, packed, LANES),
-            vm(tiles, packed, LANES),
         ),
-        name="first_step",
-    )(populations, tracer, solid_mask, inflow, wind_profile, emission)
+        (populations, tracer, solid_mask, inflow, wind_profile, emission),
+        far_args=6,
+        scratch=[vm(3, nz)] + buffers(2),
+    )
     from_south = passed_along(y_up, "gy", 1)
     from_north = passed_along(y_down, "gy", -1)
+    inner, x_up, x_down = run(
+        lambda *refs: first_inner(*refs, nz=nz),
+        (vm(UNITS, inner_tiles, extent, LANES), vm(tiles, packed, LANES), vm(tiles, packed, LANES)),
+        (populations, tracer, solid_mask, inflow, emission, winds, edge),
+        far_args=5,
+        scratch=buffers(inner_tiles),
+    )
     west = passed_along(x_up, "gx", 1)
     east = passed_along(x_down, "gx", -1)
-    sides, corner_up, corner_down = pl.pallas_call(
-        lambda *refs: turn_corner(nz, *refs),
-        out_shape=(vm(UNITS, 2, extent, LANES), vm(2, packed, LANES), vm(2, packed, LANES)),
-        name="turn_corner",
-    )(near(from_south), near(from_north))
+    sides, corner_up, corner_down = run(
+        lambda *refs: turn_corner(*refs, nz=nz),
+        (vm(UNITS, 2, extent, LANES), vm(2, packed, LANES), vm(2, packed, LANES)),
+        (from_south, from_north),
+    )
     corner_west = passed_along(corner_up, "gx", 1)
     corner_east = passed_along(corner_down, "gx", -1)
-    rows = extent + 2 * STEPS
-    return pl.pallas_call(
-        later_steps,
-        out_shape=(plain(FLOW, extent, tiles * LANES), plain(7, extent, tiles * LANES)),
-        scratch_shapes=[
-            vm(UNITS, tiles + 2, rows, LANES),
-            vm(MOVING, tiles + 2, rows, LANES),
-            vm(MOVING, tiles + 2, rows, LANES),
+    level = vm(MOVING, tiles, rows, LANES)
+    one, two, three, four, done = run(
+        lambda *refs: inner_steps(*refs, nz=nz),
+        (vm(UNITS, tiles, rows, LANES), level, level, level, vm(MOVING, inner_tiles, extent, LANES)),
+        (edge, inner, winds, west, east),
+    )
+    return run(
+        lambda *refs: outer_steps(*refs, nz=nz),
+        (
+            jax.ShapeDtypeStruct((FLOW, extent, tiles * LANES), jnp.float32),
+            jax.ShapeDtypeStruct((7, extent, tiles * LANES), jnp.float32),
+        ),
+        (one, two, three, four, done, winds, sides, corner_west, corner_east),
+        out_specs=(far, far),
+        scratch=[
+            vm(UNITS, 2, rows, LANES),
+            vm(MOVING, 4, rows, LANES),
+            vm(MOVING, 3, rows, LANES),
+            vm(MOVING, 3, rows, LANES),
+            vm(MOVING, 2, extent, LANES),
+            pltpu.SemaphoreType.DMA((2 * tiles,)),
         ],
-        name="later_steps",
-    )(near(centre), near(sides), wind_profile, near(west), near(east), near(corner_west), near(corner_east))
+    )
 
 
 def solution(mesh):
@@ -393,4 +606,5 @@
         P("gx", "gy"),
     )
     out_specs = (P(None, "gx", "gy"), P(None, "gx", "gy"))
+
     return jax.shard_map(local, mesh=mesh, in_specs=in_specs, out_specs=out_specs, check_vma=False)

time: 27.2 us -> 23.3 us (0.86)
  the two profiles are of different devices: /device:TPU:1 before, /device:TPU:0 now
where the time goes in v2:
time: 23.3 us; the launch traced here: 22.8 us
  starting transfers between devices  9.73 us (42%)
  Pallas kernels  8.39 us (36%)
  waiting for transfers between devices  4.02 us (17%)
  between operations  0.69 us (3%)
    ppermute x6, starting transfers between devices, passed_along(): lax.ppermute(shard, axis, [(i, (i + by) % length) for i in range(length)])  9.73 us
    pallas_call x5, Pallas kernels, run(): pl.pallas_call(body, out_shape=out_shape, in_specs=specs, scratch_shapes=...  8.39 us
    ppermute x6, waiting for transfers between devices, passed_along(): lax.ppermute(shard, axis, [(i, (i + by) % length) for i in range(length)])  4.02 us
  transfers between devices with their start and end apart: 6, of which 2 were waited for; matrix products, arithmetic and copies ran while one was open for 0% of the time, Pallas kernels for 20%

profile of v2, /device:TPU:0, one launch (start us, length us, event | category | flops | bytes accessed | tf_op | source)
XLA Modules:
  0.0 22.8 jit_solution(6955809498810555333)
XLA Ops:
  0.6 1.4 %shard_map.77 = (f32[29,2,16,128]{3,2,1,0:T(8,128)S(1)}, f32[3,128]{1,0:T(4,128)S(1)}, f32[23,16,128]{2,1,0:T(8,128)S(1)}, f32[23,16,128]{2,1,0:T(8,128)S(1)}) custom-call(f32[19,16,512]{2,1,0:T(8,128)} %refs_0_.1, f32[7,16,512]{2,1,0:T(8,128)} %refs_1_.1, s32[16,512]{1,0:T(8,128)} %refs_2_.1, s32[16,512]{1,0:T(8,128)} %refs_3_.1, f32[3,32]{1,0:T(4,128)} %wind.1, ...), custom_call_target="tpu_custom_call" | custom-call | tf_op jit(solution)/shard_map/pallas_call | solution.py:535
  2.0 3.0 %collective-permute-start.2 = (f32[23,16,128]{2,1,0:T(8,128)S(1)}, f32[23,16,128]{2,1,0:T(8,128)S(1)}, u32[]{:S(2)}, u32[]{:S(2)}) collective-permute-start(f32[23,16,128]{2,1,0:T(8,128)S(1)} %get-tuple-element.27), channel_id=1, source_target_pairs={{0,1},{1,2},{2,3},{3,4},{4,5},{5,6},{6,7},{7,0},{8,9},{9,10},{10,1... | collective-permute-start | bytes 565256 | tf_op jit(solution)/shard_map/ppermute | solution.py:505
  5.0 3.1 %collective-permute-start.3 = (f32[23,16,128]{2,1,0:T(8,128)S(1)}, f32[23,16,128]{2,1,0:T(8,128)S(1)}, u32[]{:S(2)}, u32[]{:S(2)}) collective-permute-start(f32[23,16,128]{2,1,0:T(8,128)S(1)} %get-tuple-element.28), channel_id=1, source_target_pairs={{0,7},{1,0},{2,1},{3,2},{4,3},{5,4},{6,5},{7,6},{8,15},{9,8},{10,9... | collective-permute-start | bytes 565256 | tf_op jit(solution)/shard_map/ppermute | solution.py:505
  8.1 1.3 %shard_map.78 = (f32[29,2,16,128]{3,2,1,0:T(8,128)S(1)}, f32[4,88,128]{2,1,0:T(8,128)S(1)}, f32[4,88,128]{2,1,0:T(8,128)S(1)}) custom-call(f32[19,16,512]{2,1,0:T(8,128)} %refs_0_.1, f32[7,16,512]{2,1,0:T(8,128)} %refs_1_.1, s32[16,512]{1,0:T(8,128)} %refs_2_.1, s32[16,512]{1,0:T(8,128)} %refs_3_.1, f32[16,512]{1,0:T(8,128)} %refs_4_.1, ...), custom_call_target="tpu_custom_call" | custom-call | tf_op jit(solution)/shard_map/pallas_call | solution.py:535
  9.5 0.1 collective-permute-start
  9.5 1.7 %collective-permute-start.1 = (f32[4,88,128]{2,1,0:T(8,128)S(1)}, f32[4,88,128]{2,1,0:T(8,128)S(1)}, u32[]{:S(2)}, u32[]{:S(2)}) collective-permute-start(f32[4,88,128]{2,1,0:T(8,128)S(1)} %get-tuple-element.21), channel_id=1, source_target_pairs={{0,24},{8,0},{16,8},{24,16},{1,25},{9,1},{17,9},{25,17},{2,26},{10... | collective-permute-start | bytes 540680 | tf_op jit(solution)/shard_map/ppermute | solution.py:505
  11.3 1.8 %collective-permute-done.2.refs_0_ = f32[23,16,128]{2,1,0:T(8,128)S(1)} collective-permute-done((f32[23,16,128]{2,1,0:T(8,128)S(1)}, f32[23,16,128]{2,1,0:T(8,128)S(1)}, u32[]{:S(2)}, u32[]{:S(2)}) %collective-permute-start.2) | collective-permute-done | bytes 188448 | tf_op jit(solution)/shard_map/ppermute | solution.py:505
  13.1 2.2 %collective-permute-done.3.refs_1_ = f32[23,16,128]{2,1,0:T(8,128)S(1)} collective-permute-done((f32[23,16,128]{2,1,0:T(8,128)S(1)}, f32[23,16,128]{2,1,0:T(8,128)S(1)}, u32[]{:S(2)}, u32[]{:S(2)}) %collective-permute-start.3) | collective-permute-done | bytes 188448 | tf_op jit(solution)/shard_map/ppermute | solution.py:505
  15.3 0.2 shard_map.80
  15.4 0.1 collective-permute-start.4
  15.5 1.7 %collective-permute-start.5 = (f32[2,88,128]{2,1,0:T(8,128)S(1)}, f32[2,88,128]{2,1,0:T(8,128)S(1)}, u32[]{:S(2)}, u32[]{:S(2)}) collective-permute-start(f32[2,88,128]{2,1,0:T(8,128)S(1)} %get-tuple-element.31), channel_id=1, source_target_pairs={{0,24},{8,0},{16,8},{24,16},{1,25},{9,1},{17,9},{25,17},{2,26},{10... | collective-permute-start | bytes 270344 | tf_op jit(solution)/shard_map/ppermute | solution.py:505
  17.2 0.0 collective-permute-done.refs_3_
  17.2 0.0 collective-permute-done.1.refs_4_
  17.2 3.0 %shard_map.79 = (f32[29,4,24,128]{3,2,1,0:T(8,128)S(1)}, f32[26,4,24,128]{3,2,1,0:T(8,128)S(1)}, f32[26,4,24,128]{3,2,1,0:T(8,128)S(1)}, f32[26,4,24,128]{3,2,1,0:T(8,128)S(1)}, f32[26,2,16,128]{3,2,1,0:T(8,128)S(1)}) custom-call(f32[29,2,16,128]{3,2,1,0:T(8,128)S(1)} %get-tuple-element.17.refs_6_.refs_0_, f32[29,2,16,128]{3,2,1,0:T(8,128)S(1)} %get-tuple-element.19.refs_1_, ...), custom_call_target="tpu_custom_call" | custom-call | tf_op jit(solution)/shard_map/pallas_call | solution.py:535
  20.2 0.0 collective-permute-done.4.refs_7_
  20.3 0.0 collective-permute-done.5.refs_8_
  20.3 2.6 %shard_map.81 = (f32[19,16,512]{2,1,0:T(8,128)}, f32[7,16,512]{2,1,0:T(8,128)}) custom-call(f32[29,4,24,128]{3,2,1,0:T(8,128)S(1)} %get-tuple-element.22.refs_0_, f32[26,4,24,128]{3,2,1,0:T(8,128)S(1)} %get-tuple-element.23.refs_1_, f32[26,4,24,128]{3,2,1,0:T(8,128)S(1)} %get-tuple-element.24.refs_2_, f32[26,4,24,128]{3,2,1,0:T(8,128)S(1)} %get-tuple-element.25.refs_3_, ...), custom_call_target="tpu_custom_call" | custom-call | tf_op jit(solution)/shard_map/pallas_call | solution.py:535
Async XLA Ops:
  2.0 11.1 %collective-permute-start.2 = (f32[23,16,128]{2,1,0:T(8,128)S(1)}, f32[23,16,128]{2,1,0:T(8,128)S(1)}, u32[]{:S(2)}, u32[]{:S(2)}) collective-permute-start(f32[23,16,128]{2,1,0:T(8,128)S(1)} %get-tuple-element.27), channel_id=1, source_target_pairs={{0,1},{1,2},{2,3},{3,4},{4,5},{5,6},{6,7},{7,0},{8,9},{9,10},{10,1... | collective-permute-start | bytes 565256 | tf_op jit(solution)/shard_map/ppermute | solution.py:505
  5.0 10.2 %collective-permute-start.3 = (f32[23,16,128]{2,1,0:T(8,128)S(1)}, f32[23,16,128]{2,1,0:T(8,128)S(1)}, u32[]{:S(2)}, u32[]{:S(2)}) collective-permute-start(f32[23,16,128]{2,1,0:T(8,128)S(1)} %get-tuple-element.28), channel_id=1, source_target_pairs={{0,7},{1,0},{2,1},{3,2},{4,3},{5,4},{6,5},{7,6},{8,15},{9,8},{10,9... | collective-permute-start | bytes 565256 | tf_op jit(solution)/shard_map/ppermute | solution.py:505
  9.5 7.8 %collective-permute-start = (f32[4,88,128]{2,1,0:T(8,128)S(1)}, f32[4,88,128]{2,1,0:T(8,128)S(1)}, u32[]{:S(2)}, u32[]{:S(2)}) collective-permute-start(f32[4,88,128]{2,1,0:T(8,128)S(1)} %get-tuple-element.20), channel_id=1, source_target_pairs={{0,8},{8,16},{16,24},{24,0},{1,9},{9,17},{17,25},{25,1},{2,10},{10... | collective-permute-start | bytes 540680 | tf_op jit(solution)/shard_map/ppermute | solution.py:505
  9.5 7.7 %collective-permute-start.1 = (f32[4,88,128]{2,1,0:T(8,128)S(1)}, f32[4,88,128]{2,1,0:T(8,128)S(1)}, u32[]{:S(2)}, u32[]{:S(2)}) collective-permute-start(f32[4,88,128]{2,1,0:T(8,128)S(1)} %get-tuple-element.21), channel_id=1, source_target_pairs={{0,24},{8,0},{16,8},{24,16},{1,25},{9,1},{17,9},{25,17},{2,26},{10... | collective-permute-start | bytes 540680 | tf_op jit(solution)/shard_map/ppermute | solution.py:505
  15.4 4.8 %collective-permute-start.4 = (f32[2,88,128]{2,1,0:T(8,128)S(1)}, f32[2,88,128]{2,1,0:T(8,128)S(1)}, u32[]{:S(2)}, u32[]{:S(2)}) collective-permute-start(f32[2,88,128]{2,1,0:T(8,128)S(1)} %get-tuple-element.30), channel_id=1, source_target_pairs={{0,8},{8,16},{16,24},{24,0},{1,9},{9,17},{17,25},{25,1},{2,10},{10... | collective-permute-start | bytes 270344 | tf_op jit(solution)/shard_map/ppermute | solution.py:505
  15.5 4.8 %collective-permute-start.5 = (f32[2,88,128]{2,1,0:T(8,128)S(1)}, f32[2,88,128]{2,1,0:T(8,128)S(1)}, u32[]{:S(2)}, u32[]{:S(2)}) collective-permute-start(f32[2,88,128]{2,1,0:T(8,128)S(1)} %get-tuple-element.31), channel_id=1, source_target_pairs={{0,24},{8,0},{16,8},{24,16},{1,25},{9,1},{17,9},{25,17},{2,26},{10... | collective-permute-start | bytes 270344 | tf_op jit(solution)/shard_map/ppermute | solution.py:505

commit v3 on v2

v3 whole, which is shorter than its diff:
```python
import math

import jax
import jax.numpy as jnp
from jax import lax
from jax.experimental import pallas as pl
from jax.experimental.pallas import tpu as pltpu
from jax.sharding import PartitionSpec as P


STEPS = 4
LANES = 128
KERNEL_BYTES = 16 * 2**20
ROWS = 8

LATTICE = (
    (0, 0, 0),
    (1, 0, 0),
    (-1, 0, 0),
    (0, 1, 0),
    (0, -1, 0),
    (0, 0, 1),
    (0, 0, -1),
    (1, 1, 0),
    (-1, -1, 0),
    (1, -1, 0),
    (-1, 1, 0),
    (1, 0, 1),
    (-1, 0, -1),
    (1, 0, -1),
    (-1, 0, 1),
    (0, 1, 1),
    (0, -1, -1),
    (0, 1, -1),
    (0, -1, 1),
)
OPPOSITE = (0, 2, 1, 4, 3, 6, 5, 8, 7, 10, 9, 12, 11, 14, 13, 16, 15, 18, 17)
BASE_RELAX = 0.6
SMAGORINSKY = 0.2
TRACER_RELAX = 0.7

FLOW = 19
MOVING = 26
SOLID, INFLOW, EMISSION = 26, 27, 28
UNITS = 29
SPEED = LATTICE + LATTICE[:7] + ((0, 0, 0),) * 3
TURNED = OPPOSITE + tuple(FLOW + k for k in OPPOSITE[:7])


def split_units(axis, sign):
    along = [u for u in range(UNITS) if SPEED[u][axis] == sign]
    still = [u for u in range(UNITS) if SPEED[u][axis] == 0]
    against = [u for u in range(UNITS) if SPEED[u][axis] == -sign]
    return along, still, against


def wall_pair(axis, sign):
    against = split_units(axis, sign)[2]
    return tuple(next(u for u in against if SPEED[u][2] == step) for step in (-1, 1))


def row_plan(sign):
    plan, offset = [], 0
    for units, depth in zip(split_units(0, sign), (STEPS, STEPS - 1, STEPS - 2)):
        for u in units:
            plan.append((u, STEPS - depth if sign > 0 else 0, depth, offset))
            offset += depth
    return plan, (offset, 1 if sign > 0 else 2), -(-(offset + 1) // ROWS) * ROWS


def pack_rows(read, store, sign, first, height):
    plan, (offset, row), _ = row_plan(sign)
    for u, low, depth, at in plan:
        store(at, depth, read(u, first + low, depth))
    floor, roof = wall_pair(0, sign)
    store(offset, 1, jnp.where(height[:1] == 0, read(floor, first + row, 1), read(roof, first + row, 1)))


def unpack_rows(read, store, sign, first):
    plan, (offset, row), _ = row_plan(sign)
    for u, low, depth, at in plan:
        store(u, first + low, read(at, depth))
    for u in wall_pair(0, sign):
        store(u, first + row, read(offset, 1))


def pack_columns(read, store, sign, lane, nz):
    along, still, against = split_units(1, sign)
    for t, u in enumerate(along):
        store(t, read(u))
    half = LANES // 2
    for t, u in enumerate(still):
        value = read(u)
        if t < 2 * len(against):
            chunk = t % 2
            other = read(against[t // 2])
            if sign > 0:
                value = jnp.where(lane < nz, pltpu.roll(other, half - nz * chunk, 1), value)
            else:
                value = jnp.where(lane >= LANES - nz, pltpu.roll(other, LANES - nz - nz * chunk, 1), value)
        elif t == 2 * len(against):
            floor, roof = wall_pair(1, sign)
            other = jnp.where(lane % nz == 0, read(floor), read(roof))
            if sign > 0:
                value = jnp.where(lane < nz, pltpu.roll(other, LANES - nz, 1), value)
            else:
                value = jnp.where(lane >= LANES - nz, pltpu.roll(other, nz, 1), value)
        store(len(along) + t, value)


def unpack_columns(read, store, sign, lane, nz):
    along, still, against = split_units(1, sign)
    for t, u in enumerate(along):
        store(u, read(t))
    base = len(along)
    for t, u in enumerate(still):
        store(u, read(base + t))
    half = LANES // 2
    for t, u in enumerate(against):
        first, second = read(base + 2 * t), read(base + 2 * t + 1)
        if sign > 0:
            value = jnp.where(lane < LANES - nz, pltpu.roll(first, half, 1), pltpu.roll(second, half + nz, 1))
        else:
            value = jnp.where(lane < nz, pltpu.roll(first, nz, 1), pltpu.roll(second, 2 * nz, 1))
        if u in wall_pair(1, sign):
            walls = read(base + 2 * len(against))
            if sign > 0:
                value = jnp.where(lane < half, pltpu.roll(walls, nz, 1), value)
            else:
                value = jnp.where(lane >= half, pltpu.roll(walls, LANES - nz, 1), value)
        store(u, value)


def relax(h, q, solid, inflow, emission, wind):
    w_rest, w_axis, w_diag = 1.0 / 3.0, 1.0 / 18.0, 1.0 / 36.0
    total = {k: h[k] + h[k + 1] for k in range(1, 19, 2)}
    gap = {k: h[k] - h[k + 1] for k in range(1, 19, 2)}
    xy, xz, yz = total[7] + total[9], total[11] + total[13], total[15] + total[17]
    axes = total[1] + total[3] + total[5]
    density = w_rest * h[0] + w_axis * axes + w_diag * (xy + xz + yz)
    ux = w_axis * gap[1] + w_diag * (gap[7] + gap[9] + gap[11] + gap[13])
    uy = w_axis * gap[3] + w_diag * (gap[7] - gap[9] + gap[15] + gap[17])
    uz = w_axis * gap[5] + w_diag * (gap[11] - gap[13] + gap[15] - gap[17])
    uxx, uyy, uzz = ux * ux, uy * uy, uz * uz
    third = w_rest * density
    pxx = w_axis * total[1] + w_diag * (xy + xz) - third - uxx
    pyy = w_axis * total[3] + w_diag * (xy + yz) - third - uyy
    pzz = w_axis * total[5] + w_diag * (xz + yz) - third - uzz
    pxy = w_diag * (total[7] - total[9]) - ux * uy
    pxz = w_diag * (total[11] - total[13]) - ux * uz
    pyz = w_diag * (total[15] - total[17]) - uy * uz
    cross = pxy * pxy + pxz * pxz + pyz * pyz
    contraction = pxx * pxx + pyy * pyy + pzz * pzz + (cross + cross)
    strength = 18.0 * math.sqrt(2.0) * SMAGORINSKY * SMAGORINSKY
    relax_time = 0.5 * (BASE_RELAX + jnp.sqrt(BASE_RELAX * BASE_RELAX + strength * jnp.sqrt(contraction)))
    rate = 1.0 / relax_time

    keep = 1.0 - 1.0 / TRACER_RELAX
    amount = 0.25 * q[0] + 0.125 * ((q[1] + q[2]) + (q[3] + q[4]) + (q[5] + q[6]))
    source = jnp.where(inflow, 0.0, amount * (1.0 / TRACER_RELAX))
    hold = jnp.where(inflow, 0.0, keep)
    level = source + jnp.where(inflow, 0.0, emission)
    push = 4.0 * source
    traced = [None] * 7
    traced[0] = jnp.where(solid, q[0], hold * q[0] + level)
    for k, speed in ((1, ux), (3, uy), (5, uz)):
        shift = push * speed
        traced[k] = jnp.where(solid, q[k + 1], hold * q[k] + (level + shift))
        traced[k + 1] = jnp.where(solid, q[k], hold * q[k + 1] + (level - shift))

    rate = jnp.where(inflow, 1.0, rate)
    density = jnp.where(inflow, 1.0, density)
    ux, uy, uz = (jnp.where(inflow, w, u) for w, u in zip(wind, (ux, uy, uz)))
    rest = 1.0 - rate
    square = ux * ux + uy * uy + uz * uz
    base = rate * (density - 1.5 * square)
    linear = 3.0 * rate
    quadratic = 4.5 * rate
    relaxed = [None] * 19
    relaxed[0] = jnp.where(solid, h[0], rest * h[0] + base)
    along = {1: ux, 3: uy, 5: uz, 7: ux + uy, 9: ux - uy, 11: ux + uz, 13: ux - uz, 15: uy + uz, 17: uy - uz}
    for k, speed in along.items():
        even = base + quadratic * speed * speed
        odd = linear * speed
        relaxed[k] = jnp.where(solid, h[k + 1], rest * h[k] + (even + odd))
        relaxed[k + 1] = jnp.where(solid, h[k], rest * h[k + 1] + (even - odd))
    return relaxed + traced


def by_side(axis, body, near, far):
    even = lax.axis_index(axis) % 2 == 0
    pl.when(even)(lambda: body(near, far))
    pl.when(jnp.logical_not(even))(lambda: body(far, near))


def lane_index():
    return lax.broadcasted_iota(jnp.int32, (ROWS, LANES), 1)


def wind_tiles(wind):
    return [jnp.broadcast_to(wind[a : a + 1, :], (ROWS, LANES)) for a in range(3)]


def start_all(copies, sems):
    started = [pltpu.make_async_copy(src, dst, sems.at[n]) for n, (src, dst) in enumerate(copies)]
    for copy in started:
        copy.start()
    return started


def relax_own(cells, winds, store, rows):
    populations, tracer, solid, inflow, emission = cells
    h = [populations[k, rows, :] for k in range(FLOW)]
    q = [tracer[k, rows, :] for k in range(7)]
    built, held, emitted = solid[rows, :], inflow[rows, :], emission[rows, :]
    out = relax(h, q, built == 1, held == 1, emitted, winds)
    for u, value in enumerate(out + [built.astype(jnp.float32), held.astype(jnp.float32), emitted]):
        store(u, value)


def load_tiles(arrays, buffers, columns, sems, extra=()):
    copies = list(extra)
    for n, j in enumerate(columns):
        lanes = pl.ds(j * LANES, LANES)
        for array, buffer in zip(arrays, buffers):
            src = array.at[:, :, lanes] if len(array.shape) == 3 else array.at[:, lanes]
            copies.append((src, buffer.at[n]))
    started = start_all(copies, sems)
    count = len(arrays)
    own = [started[len(extra) + n * count : len(extra) + (n + 1) * count] for n in range(len(columns))]
    return started[: len(extra)], own


def first_edges(
    populations, tracer, solid, inflow, wind, emission, one, winds, y_near, y_far,
    wind_in, pop_in, tracer_in, solid_in, inflow_in, emission_in, sems,
):
    extent = populations.shape[1]
    tiles = populations.shape[2] // LANES
    nz = wind.shape[1]
    lane = lane_index()
    buffers = (pop_in, tracer_in, solid_in, inflow_in, emission_in)
    common, own = load_tiles(
        (populations, tracer, solid, inflow, emission), buffers, (tiles - 1, 0), sems, ((wind, wind_in),)
    )
    for copy in common:
        copy.wait()
    winds[...] = jnp.concatenate([wind_in[...]] * (LANES // nz), axis=1)
    wind_values = wind_tiles(winds)
    for n, at in enumerate((tiles, 1)):
        for copy in own[n]:
            copy.wait()
        cells = [b.at[n] for b in buffers]
        for r in range(0, extent, ROWS):
            rows = slice(r, r + ROWS)

            def keep(u, value, at=at, r=r):
                one[u, at, STEPS + r : STEPS + r + ROWS, :] = value

            relax_own(cells, wind_values, keep, rows)

    def pack(up, down):
        for at, sign, target in ((tiles, 1, up), (1, -1, down)):
            for r in range(0, extent, ROWS):
                def send(t, value, target=target, r=r):
                    target[t, r : r + ROWS, :] = value

                pack_columns(
                    lambda u, at=at, r=r: one[u, at, STEPS + r : STEPS + r + ROWS, :], send, sign, lane, nz
                )

    by_side("gy", pack, y_near, y_far)


def first_inner(
    populations, tracer, solid, inflow, emission, winds, _, one, x_near, x_far,
    pop_in, tracer_in, solid_in, inflow_in, emission_in, sems, *, nz,
):
    extent = populations.shape[1]
    tiles = populations.shape[2] // LANES
    height = lane_index() % nz
    buffers = (pop_in, tracer_in, solid_in, inflow_in, emission_in)
    columns = tuple(range(1, tiles - 1))
    _, own = load_tiles((populations, tracer, solid, inflow, emission), buffers, columns, sems)
    wind_values = wind_tiles(winds)

    for n, j in enumerate(columns):
        for copy in own[n]:
            copy.wait()
        for r in range(0, extent, ROWS):
            rows = slice(r, r + ROWS)

            def keep(u, value, j=j, r=r):
                one[u, j + 1, STEPS + r : STEPS + r + ROWS, :] = value

            relax_own([b.at[n] for b in buffers], wind_values, keep, rows)
    by_side("gx", lambda up, down: pack_sides(one, range(1, tiles + 1), up, down, extent, height), x_near, x_far)


def pack_sides(one, columns, up, down, extent, height):
    for at, c in enumerate(columns):
        for sign, target, first in ((1, up, extent), (-1, down, STEPS)):
            def store(offset, depth, value, target=target, at=at):
                target[at, offset : offset + depth, :] = value

            pack_rows(lambda u, low, depth, c=c: one[u, c, low : low + depth, :], store, sign, first, height)


def turn_corner(from_near, from_far, _, one, x_near, x_far, *, nz):
    wide = one.shape[1]
    extent = one.shape[2] - 2 * STEPS
    lane = lane_index()
    height = lane % nz

    def unpack(north, south):
        for sign, source, at in ((1, south, 0), (-1, north, wide - 1)):
            for r in range(0, extent, ROWS):
                def store(u, value, at=at, r=r):
                    one[u, at, STEPS + r : STEPS + r + ROWS, :] = value

                unpack_columns(lambda t, source=source, r=r: source[t, r : r + ROWS, :], store, sign, lane, nz)

    by_side("gy", unpack, from_near, from_far)
    by_side("gx", lambda up, down: pack_sides(one, (0, wide - 1), up, down, extent, height), x_near, x_far)


class Mover:
    def __init__(self, nz):
        lane = lane_index()
        height = lane % nz
        self.nz = nz
        self.from_part = [None] + [lane >= part * nz for part in range(1, LANES // nz)]
        self.floor, self.roof = height == 0, height == nz - 1

    def merge(self, read, columns):
        value = read(columns[0])
        for part in range(1, len(columns)):
            if columns[part] != columns[part - 1]:
                value = jnp.where(self.from_part[part], read(columns[part]), value)
        return value

    def pull(self, read, parts, u):
        step_x, step_y, step_z = SPEED[u]
        value = self.merge(lambda c: read(u, c, step_x), parts[step_y])
        shift = (self.nz * step_y + step_z) % LANES
        if shift:
            value = pltpu.roll(value, shift, 1)
        if step_z:
            own = self.merge(lambda c: read(TURNED[u], c, 0), parts[0])
            value = jnp.where(self.floor if step_z == 1 else self.roof, own, value)
        return value


class Block:
    def __init__(self, one, two, three, four, done, winds, nz):
        self.levels = (None, one, two, three, four)
        self.done = done
        self.tiles = done.shape[1]
        self.extent = done.shape[2]
        self.last = self.tiles + 1
        self.both = self.tiles + 2
        self.count = LANES // nz
        self.mover = Mover(nz)
        self.winds = wind_tiles(winds)
        self.upper = lax.broadcasted_iota(jnp.int32, (ROWS, LANES), 0) < ROWS // 2

    def centre(self, step):
        low, high = STEPS + step, STEPS + self.extent - step
        return list(range(low, high - ROWS, ROWS)) + [high - ROWS]

    def seam(self, step):
        return (step, STEPS + self.extent - step)

    def read(self, level, u, c, place, back=0):
        ref = self.levels[level]
        if isinstance(place, tuple):
            low, high = place[0] - back, place[1] - back - ROWS // 2
            return jnp.where(self.upper, ref[u, c, low : low + ROWS, :], ref[u, c, high : high + ROWS, :])
        return ref[u, c, place - back : place - back + ROWS, :]

    def write(self, ref, u, c, place, value, lift=0):
        if isinstance(place, tuple):
            half = ROWS // 2
            ref[u, c, place[0] - lift : place[0] - lift + half, :] = value[:half]
            ref[u, c, place[1] - lift : place[1] - lift + half, :] = value[half:]
        else:
            ref[u, c, place - lift : place - lift + ROWS, :] = value

    def sources(self, level, c, before, after):
        tiles, last, both, count = self.tiles, self.last, self.both, self.count
        half = count // 2
        if c == both and level < 3:
            return {
                0: [last] * half + [0] * (count - half),
                1: [last] * (half - 1) + [0] * (count - half) + [tiles],
                -1: [1] + [last] * half + [0] * (count - half - 1),
            }
        return {0: [c] * count, 1: [c] * (count - 1) + [before], -1: [after] + [c] * (count - 1)}

    def around(self, level, c, margins):
        if not margins:
            return max(c - 1, 1), min(c + 1, self.tiles)
        if c == self.both:
            return self.tiles, 1
        before = self.both if c == 1 and level > 2 else max(c - 1, 0)
        after = self.both if c == self.tiles and level > 2 else min(c + 1, self.last)
        return before, after

    def pull(self, level, c, place, margins):
        parts = self.sources(level, c, *self.around(level, c, margins))
        return [
            self.mover.pull(lambda v, at, back: self.read(level, v, at, place, back), parts, u) for u in range(MOVING)
        ]

    def relax(self, step, c, place, margins):
        moved = self.pull(step, c, place, margins)
        here = self.sources(1, c, c, c)[0]
        solid, inflow, emission = (
            self.mover.merge(lambda at, u=u: self.read(1, u, at, place), here) for u in (SOLID, INFLOW, EMISSION)
        )
        out = relax(moved[:FLOW], moved[FLOW:], solid == 1.0, inflow == 1.0, emission, self.winds)
        for u in range(MOVING):
            self.write(self.levels[step + 1], u, c, place, out[u])

    def finish(self, c, place, margins):
        for u, value in enumerate(self.pull(STEPS, c, place, margins)):
            self.write(self.done, u, c - 1, place, value, STEPS)

    def steps(self, columns, places, margins):
        for step in range(1, STEPS):
            for c in columns(step):
                for place in places(step):
                    self.relax(step, c, place, margins)

    def inner(self, places):
        self.steps(lambda step: range(1, self.tiles + 1), places, False)
        for c in range(2, self.tiles):
            for place in places(STEPS):
                self.finish(c, place, False)

    def outer(self, places):
        self.steps(
            lambda step: (0, 1, self.tiles, self.last) if step == 1 else (self.both, 1, self.tiles), places, True
        )
        for c in (1, self.tiles):
            for place in places(STEPS):
                self.finish(c, place, True)


def inner_centre(winds, _, one, two, three, four, done, *, nz):
    block = Block(one, two, three, four, done, winds, nz)
    block.inner(block.centre)


def inner_seam(winds, near, far, *refs, nz):
    one, two, three, four, done = refs[5:]
    block = Block(one, two, three, four, done, winds, nz)
    columns = range(1, block.tiles + 1)
    by_side("gx", lambda east, west: fill_rows(one, columns, west, east, block.extent), near, far)
    block.inner(lambda step: [block.seam(step)])


def fill_rows(one, columns, west, east, extent):
    for at, c in enumerate(columns):
        for sign, source, first in ((1, west, 0), (-1, east, STEPS + extent)):
            def fill(u, row, value, c=c):
                one[u, c, row : row + value.shape[0], :] = value

            unpack_rows(
                lambda offset, depth, source=source, at=at: source[at, offset : offset + depth, :], fill, sign, first
            )


def outer_centre(winds, *refs, nz):
    block = Block(*refs[5:], winds, nz)
    block.outer(block.centre)


def outer_seam(winds, near, far, *refs, nz):
    one, two, three, four, done, flow_out, tracer_out, sems = refs[5:]
    block = Block(one, two, three, four, done, winds, nz)
    copies = []

    def write_out(j):
        lanes = pl.ds(j * LANES, LANES)
        for first, number, target in ((0, FLOW, flow_out), (FLOW, 7, tracer_out)):
            copy = pltpu.make_async_copy(
                done.at[pl.ds(first, number), j], target.at[:, :, lanes], sems.at[len(copies)]
            )
            copy.start()
            copies.append(copy)

    for j in range(1, block.tiles - 1):
        write_out(j)
    columns = (0, block.last)
    by_side("gx", lambda east, west: fill_rows(one, columns, west, east, block.extent), near, far)
    block.steps(
        lambda step: (0, 1, block.tiles, block.last) if step == 1 else (block.both, 1, block.tiles),
        lambda step: [block.seam(step)],
        True,
    )
    for c in (1, block.tiles):
        block.finish(c, block.seam(STEPS), True)
        write_out(c - 1)
    for copy in copies:
        copy.wait()


def swapped(shard, axis, start):
    length = lax.axis_size(axis)
    pairs = [((i + start) % length, ((i ^ 1) + start) % length) for i in range(length)]
    return lax.ppermute(shard, axis, pairs)


def local(populations, tracer, solid_mask, inflow, wind_profile, emission):
    extent = populations.shape[1]
    tiles = populations.shape[2] // LANES
    nz = wind_profile.shape[1]
    inner_tiles = tiles - 2
    along, still, _ = split_units(1, 1)
    messages = len(along) + len(still)
    packed = row_plan(1)[2]
    rows = extent + 2 * STEPS
    vm = lambda *shape: pltpu.VMEM(shape, jnp.float32)
    far = pl.BlockSpec(memory_space=pltpu.HBM)
    close = pl.BlockSpec(memory_space=pltpu.VMEM)

    def buffers(number):
        return [
            vm(number, FLOW, extent, LANES),
            vm(number, 7, extent, LANES),
            pltpu.VMEM((number, extent, LANES), jnp.int32),
            pltpu.VMEM((number, extent, LANES), jnp.int32),
            vm(number, extent, LANES),
            pltpu.SemaphoreType.DMA((5 * number + 1,)),
        ]

    def run(body, out_shape, args, far_args=0, out_specs=None, scratch=(), aliases=None):
        specs = [far] * far_args + [close] * (len(args) - far_args)
        args = tuple(
            pltpu.with_memory_space_constraint(a, pltpu.HBM if n < far_args else pltpu.VMEM) for n, a in enumerate(args)
        )
        options = {} if out_specs is None else {"out_specs": out_specs}
        return pl.pallas_call(
            body,
            out_shape=out_shape,
            in_specs=specs,
            scratch_shapes=list(scratch),
            input_output_aliases=aliases or {},
            compiler_params=pltpu.CompilerParams(vmem_limit_bytes=KERNEL_BYTES),
            **options,
        )(*args)

    first = vm(UNITS, tiles + 2, rows, LANES)
    levels = (first, vm(MOVING, tiles + 2, rows, LANES)) + (vm(MOVING, tiles + 3, rows, LANES),) * 2
    levels += (vm(MOVING, tiles, extent, LANES),)
    one, winds, y_near, y_far = run(
        first_edges,
        (first, vm(3, LANES), vm(messages, extent, LANES), vm(messages, extent, LANES)),
        (populations, tracer, solid_mask, inflow, wind_profile, emission),
        far_args=6,
        scratch=[vm(3, nz)] + buffers(2),
    )
    y_near = swapped(y_near, "gy", 0)
    y_far = swapped(y_far, "gy", 1)
    one, x_near, x_far = run(
        lambda *refs: first_inner(*refs, nz=nz),
        (first, vm(tiles, packed, LANES), vm(tiles, packed, LANES)),
        (populations, tracer, solid_mask, inflow, emission, winds, one),
        far_args=5,
        scratch=buffers(inner_tiles),
        aliases={6: 0},
    )
    x_near = swapped(x_near, "gx", 0)
    x_far = swapped(x_far, "gx", 1)
    state = run(lambda *refs: inner_centre(*refs, nz=nz), levels, (winds, one), aliases={1: 0})
    one, corner_near, corner_far = run(
        lambda *refs: turn_corner(*refs, nz=nz),
        (first, vm(2, packed, LANES), vm(2, packed, LANES)),
        (y_near, y_far, state[0]),
        aliases={2: 0},
    )
    corner_near = swapped(corner_near, "gx", 0)
    corner_far = swapped(corner_far, "gx", 1)
    state = run(
        lambda *refs: inner_seam(*refs, nz=nz),
        levels,
        (winds, x_near, x_far, one, *state[1:]),
        aliases={3 + n: n for n in range(5)},
    )
    state = run(lambda *refs: outer_centre(*refs, nz=nz), levels, (winds, *state), aliases={1 + n: n for n in range(5)})
    out = run(
        lambda *refs: outer_seam(*refs, nz=nz),
        levels
        + (
            jax.ShapeDtypeStruct((FLOW, extent, tiles * LANES), jnp.float32),
            jax.ShapeDtypeStruct((7, extent, tiles * LANES), jnp.float32),
        ),
        (winds, corner_near, corner_far, *state),
        out_specs=(close,) * 5 + (far, far),
        scratch=[pltpu.SemaphoreType.DMA((2 * tiles,))],
        aliases={3 + n: n for n in range(5)},
    )
    return out[5], out[6]


def solution(mesh):
    in_specs = (
        P(None, "gx", "gy"),
        P(None, "gx", "gy"),
        P("gx", "gy"),
        P("gx", "gy"),
        P(),
        P("gx", "gy"),
    )
    out_specs = (P(None, "gx", "gy"), P(None, "gx", "gy"))

    return jax.shard_map(local, mesh=mesh, in_specs=in_specs, out_specs=out_specs, check_vma=False)
```

time: 23.3 us -> 20.5 us (0.88); the launches traced: 22.8 us -> 20.4 us
  waiting for transfers between devices: 4.02 us -> 1.34 us
  starting transfers between devices: 9.73 us -> 10 us
    ppermute x6, waiting for transfers between devices: 4.02 us -> 1.34 us  [swapped(): return lax.ppermute(shard, axis, pairs)]
    ppermute x6, starting transfers between devices: 9.73 us -> 10 us  [swapped(): return lax.ppermute(shard, axis, pairs)]
    pallas_call x5 -> x7, Pallas kernels: 8.39 us -> 8.28 us  [run(): pl.pallas_call(body, out_shape=out_shape, in_specs=specs, scratch_shapes=...]
  transfers between devices with their start and end apart: 6 -> 6, of which waited for: 2 -> 2; matrix products, arithmetic and copies ran while one was open for 0% -> 0% of each run, Pallas kernels for 20% -> 25%
where the time goes in v3:
time: 20.5 us; the launch traced here: 20.4 us
  starting transfers between devices  10 us (49%)
  Pallas kernels  8.28 us (40%)
  waiting for transfers between devices  1.34 us (7%)
  between operations  0.7 us (3%)
    ppermute x6, starting transfers between devices, swapped(): return lax.ppermute(shard, axis, pairs)  10 us
    pallas_call x7, Pallas kernels, run(): pl.pallas_call(body, out_shape=out_shape, in_specs=specs, scratch_shapes=...  8.28 us
    ppermute x6, waiting for transfers between devices, swapped(): return lax.ppermute(shard, axis, pairs)  1.34 us
  transfers between devices with their start and end apart: 6, of which 2 were waited for; matrix products, arithmetic and copies ran while one was open for 0% of the time, Pallas kernels for 25%

profile of v3, /device:TPU:0, one launch (start us, length us, event | category | flops | bytes accessed | tf_op | source)
XLA Modules:
  0.0 20.4 jit_solution(14473910595252374748)
XLA Ops:
  0.6 1.4 %shard_map.77 = (f32[29,6,24,128]{3,2,1,0:T(8,128)S(1)}, f32[3,128]{1,0:T(4,128)S(1)}, f32[23,16,128]{2,1,0:T(8,128)S(1)}, f32[23,16,128]{2,1,0:T(8,128)S(1)}) custom-call(f32[19,16,512]{2,1,0:T(8,128)} %refs_0_.1, f32[7,16,512]{2,1,0:T(8,128)} %refs_1_.1, s32[16,512]{1,0:T(8,128)} %refs_2_.1, s32[16,512]{1,0:T(8,128)} %refs_3_.1, f32[3,32]{1,0:T(4,128)} %wind.1, ...), custom_call_target="tpu_custom_call" | custom-call | tf_op jit(solution)/shard_map/pallas_call | solution.py:544
  2.0 3.1 %collective-permute-start = (f32[23,16,128]{2,1,0:T(8,128)S(1)}, f32[23,16,128]{2,1,0:T(8,128)S(1)}, u32[]{:S(2)}, u32[]{:S(2)}) collective-permute-start(f32[23,16,128]{2,1,0:T(8,128)S(1)} %get-tuple-element.30), channel_id=1, source_target_pairs={{0,1},{1,0},{2,3},{3,2},{4,5},{5,4},{6,7},{7,6},{8,9},{9,8},{10,11... | collective-permute-start | bytes 565256 | tf_op jit(solution)/shard_map/ppermute | solution.py:512
  5.1 3.5 %collective-permute-start.1 = (f32[23,16,128]{2,1,0:T(8,128)S(1)}, f32[23,16,128]{2,1,0:T(8,128)S(1)}, u32[]{:S(2)}, u32[]{:S(2)}) collective-permute-start(f32[23,16,128]{2,1,0:T(8,128)S(1)} %get-tuple-element.31), channel_id=1, source_target_pairs={{1,2},{2,1},{3,4},{4,3},{5,6},{6,5},{7,0},{0,7},{9,10},{10,9},{11,... | collective-permute-start | bytes 565256 | tf_op jit(solution)/shard_map/ppermute | solution.py:512
  8.7 1.4 %shard_map.78 = (f32[29,6,24,128]{3,2,1,0:T(8,128)S(1)}, f32[4,88,128]{2,1,0:T(8,128)S(1)}, f32[4,88,128]{2,1,0:T(8,128)S(1)}) custom-call(f32[19,16,512]{2,1,0:T(8,128)} %refs_0_.1, f32[7,16,512]{2,1,0:T(8,128)} %refs_1_.1, s32[16,512]{1,0:T(8,128)} %refs_2_.1, s32[16,512]{1,0:T(8,128)} %refs_3_.1, ...), custom_call_target="tpu_custom_call", output_to_operand_aliasing={{0}: (6, {})} | custom-call | tf_op jit(solution)/shard_map/pallas_call | solution.py:544
  10.0 0.1 collective-permute-start.4
  10.1 1.6 %collective-permute-start.5 = (f32[4,88,128]{2,1,0:T(8,128)S(1)}, f32[4,88,128]{2,1,0:T(8,128)S(1)}, u32[]{:S(2)}, u32[]{:S(2)}) collective-permute-start(f32[4,88,128]{2,1,0:T(8,128)S(1)} %get-tuple-element.38), channel_id=1, source_target_pairs={{8,16},{16,8},{24,0},{0,24},{9,17},{17,9},{25,1},{1,25},{10,18},{1... | collective-permute-start | bytes 540680 | tf_op jit(solution)/shard_map/ppermute | solution.py:512
  11.7 1.4 %shard_map.79 = (f32[29,6,24,128]{3,2,1,0:T(8,128)S(1)}, f32[26,6,24,128]{3,2,1,0:T(8,128)S(1)}, f32[26,7,24,128]{3,2,1,0:T(8,128)S(1)}, f32[26,7,24,128]{3,2,1,0:T(8,128)S(1)}, f32[26,4,16,128]{3,2,1,0:T(8,128)S(1)}) custom-call(f32[3,128]{1,0:T(4,128)S(1)} %get-tuple-element.29.refs_5_.refs_0_, ...), custom_call_target="tpu_custom_call", output_to_operand_aliasing={{0}: (1, {})} | custom-call | tf_op jit(solution)/shard_map/pallas_call | solution.py:544
  13.1 0.0 collective-permute-done.refs_0_
  13.1 0.9 %collective-permute-done.1.refs_1_ = f32[23,16,128]{2,1,0:T(8,128)S(1)} collective-permute-done((f32[23,16,128]{2,1,0:T(8,128)S(1)}, f32[23,16,128]{2,1,0:T(8,128)S(1)}, u32[]{:S(2)}, u32[]{:S(2)}) %collective-permute-start.1) | collective-permute-done | bytes 188448 | tf_op jit(solution)/shard_map/ppermute | solution.py:512
  14.0 0.2 shard_map.80
  14.2 0.1 collective-permute-start.2
  14.3 1.7 %collective-permute-start.3 = (f32[2,88,128]{2,1,0:T(8,128)S(1)}, f32[2,88,128]{2,1,0:T(8,128)S(1)}, u32[]{:S(2)}, u32[]{:S(2)}) collective-permute-start(f32[2,88,128]{2,1,0:T(8,128)S(1)} %get-tuple-element.36), channel_id=1, source_target_pairs={{8,16},{16,8},{24,0},{0,24},{9,17},{17,9},{25,1},{1,25},{10,18},{1... | collective-permute-start | bytes 270344 | tf_op jit(solution)/shard_map/ppermute | solution.py:512
  16.0 0.0 collective-permute-done.4.refs_1_
  16.0 0.4 %collective-permute-done.5.refs_2_ = f32[4,88,128]{2,1,0:T(8,128)S(1)} collective-permute-done((f32[4,88,128]{2,1,0:T(8,128)S(1)}, f32[4,88,128]{2,1,0:T(8,128)S(1)}, u32[]{:S(2)}, u32[]{:S(2)}) %collective-permute-start.5) | collective-permute-done | bytes 180256 | tf_op jit(solution)/shard_map/ppermute | solution.py:512
  16.4 1.0 %shard_map.81 = (f32[29,6,24,128]{3,2,1,0:T(8,128)S(1)}, f32[26,6,24,128]{3,2,1,0:T(8,128)S(1)}, f32[26,7,24,128]{3,2,1,0:T(8,128)S(1)}, f32[26,7,24,128]{3,2,1,0:T(8,128)S(1)}, f32[26,4,16,128]{3,2,1,0:T(8,128)S(1)}) custom-call(f32[3,128]{1,0:T(4,128)S(1)} %get-tuple-element.29.refs_, ...), custom_call_target="tpu_custom_call", output_to_operand_aliasing={{0}: (3, {}), {1}: (4, {}), {2}: (5, {}), {3}: (6, {}), {4}... | custom-call | tf_op jit(solution)/shard_map/pallas_call | solution.py:544
  17.4 1.2 %shard_map.82 = (f32[29,6,24,128]{3,2,1,0:T(8,128)S(1)}, f32[26,6,24,128]{3,2,1,0:T(8,128)S(1)}, f32[26,7,24,128]{3,2,1,0:T(8,128)S(1)}, f32[26,7,24,128]{3,2,1,0:T(8,128)S(1)}, f32[26,4,16,128]{3,2,1,0:T(8,128)S(1)}) custom-call(f32[3,128]{1,0:T(4,128)S(1)} %get-tuple-element.29.refs_, ...), custom_call_target="tpu_custom_call", output_to_operand_aliasing={{0}: (1, {}), {1}: (2, {}), {2}: (3, {}), {3}: (4, {}), {4}... | custom-call | tf_op jit(solution)/shard_map/pallas_call | solution.py:544
  18.6 0.0 collective-permute-done.2.refs_1_
  18.6 0.0 collective-permute-done.3.refs_2_
  18.6 1.7 %shard_map.83 = (f32[29,6,24,128]{3,2,1,0:T(8,128)S(1)}, f32[26,6,24,128]{3,2,1,0:T(8,128)S(1)}, f32[26,7,24,128]{3,2,1,0:T(8,128)S(1)}, f32[26,7,24,128]{3,2,1,...) custom-call(f32[3,128]{1,0:T(4,128)S(1)} %get-tuple-element.29.refs_, ...), custom_call_target="tpu_custom_call", output_to_operand_aliasing={{0}: (3, {}), {1}: (4, {}), {2}: (5, {}), {3}: (6, {}), {4}... | custom-call | tf_op jit(solution)/shard_map/pallas_call | solution.py:544
Async XLA Ops:
  2.0 11.1 %collective-permute-start = (f32[23,16,128]{2,1,0:T(8,128)S(1)}, f32[23,16,128]{2,1,0:T(8,128)S(1)}, u32[]{:S(2)}, u32[]{:S(2)}) collective-permute-start(f32[23,16,128]{2,1,0:T(8,128)S(1)} %get-tuple-element.30), channel_id=1, source_target_pairs={{0,1},{1,0},{2,3},{3,2},{4,5},{5,4},{6,7},{7,6},{8,9},{9,8},{10,11... | collective-permute-start | bytes 565256 | tf_op jit(solution)/shard_map/ppermute | solution.py:512
  5.1 8.9 %collective-permute-start.1 = (f32[23,16,128]{2,1,0:T(8,128)S(1)}, f32[23,16,128]{2,1,0:T(8,128)S(1)}, u32[]{:S(2)}, u32[]{:S(2)}) collective-permute-start(f32[23,16,128]{2,1,0:T(8,128)S(1)} %get-tuple-element.31), channel_id=1, source_target_pairs={{1,2},{2,1},{3,4},{4,3},{5,6},{6,5},{7,0},{0,7},{9,10},{10,9},{11,... | collective-permute-start | bytes 565256 | tf_op jit(solution)/shard_map/ppermute | solution.py:512
  10.0 6.0 %collective-permute-start.4 = (f32[4,88,128]{2,1,0:T(8,128)S(1)}, f32[4,88,128]{2,1,0:T(8,128)S(1)}, u32[]{:S(2)}, u32[]{:S(2)}) collective-permute-start(f32[4,88,128]{2,1,0:T(8,128)S(1)} %get-tuple-element.37), channel_id=1, source_target_pairs={{0,8},{8,0},{16,24},{24,16},{1,9},{9,1},{17,25},{25,17},{2,10},{10... | collective-permute-start | bytes 540680 | tf_op jit(solution)/shard_map/ppermute | solution.py:512
  10.1 6.3 %collective-permute-start.5 = (f32[4,88,128]{2,1,0:T(8,128)S(1)}, f32[4,88,128]{2,1,0:T(8,128)S(1)}, u32[]{:S(2)}, u32[]{:S(2)}) collective-permute-start(f32[4,88,128]{2,1,0:T(8,128)S(1)} %get-tuple-element.38), channel_id=1, source_target_pairs={{8,16},{16,8},{24,0},{0,24},{9,17},{17,9},{25,1},{1,25},{10,18},{1... | collective-permute-start | bytes 540680 | tf_op jit(solution)/shard_map/ppermute | solution.py:512
  14.2 4.4 %collective-permute-start.2 = (f32[2,88,128]{2,1,0:T(8,128)S(1)}, f32[2,88,128]{2,1,0:T(8,128)S(1)}, u32[]{:S(2)}, u32[]{:S(2)}) collective-permute-start(f32[2,88,128]{2,1,0:T(8,128)S(1)} %get-tuple-element.35), channel_id=1, source_target_pairs={{0,8},{8,0},{16,24},{24,16},{1,9},{9,1},{17,25},{25,17},{2,10},{10... | collective-permute-start | bytes 270344 | tf_op jit(solution)/shard_map/ppermute | solution.py:512
  14.3 4.4 %collective-permute-start.3 = (f32[2,88,128]{2,1,0:T(8,128)S(1)}, f32[2,88,128]{2,1,0:T(8,128)S(1)}, u32[]{:S(2)}, u32[]{:S(2)}) collective-permute-start(f32[2,88,128]{2,1,0:T(8,128)S(1)} %get-tuple-element.36), channel_id=1, source_target_pairs={{8,16},{16,8},{24,0},{0,24},{9,17},{17,9},{25,1},{1,25},{10,18},{1... | collective-permute-start | bytes 270344 | tf_op jit(solution)/shard_map/ppermute | solution.py:512

commit v4 on v3

--- a/solution.py
+++ b/solution.py
@@ -84,51 +84,72 @@
         store(u, first + row, read(offset, 1))
 
 
+def message_plan(sign):
+    along, still, against = split_units(1, sign)
+    riders = [(u, chunk) for u in against for chunk in range(2)] + [(None, 0)]
+    carried = []
+    for unit in still:
+        fit = next((r for r in riders if (0 if r[0] is None else SPEED[r[0]][0]) == SPEED[unit][0]), None)
+        carried.append(fit)
+        if fit is not None:
+            riders.remove(fit)
+    return along, still, carried
+
+
 def pack_columns(read, store, sign, lane, nz):
-    along, still, against = split_units(1, sign)
+    along, still, carried = message_plan(sign)
     for t, u in enumerate(along):
         store(t, read(u))
     half = LANES // 2
-    for t, u in enumerate(still):
+    for t, (u, rider) in enumerate(zip(still, carried)):
         value = read(u)
-        if t < 2 * len(against):
-            chunk = t % 2
-            other = read(against[t // 2])
-            if sign > 0:
-                value = jnp.where(lane < nz, pltpu.roll(other, half - nz * chunk, 1), value)
+        if rider is not None:
+            unit, chunk = rider
+            if unit is None:
+                floor, roof = wall_pair(1, sign)
+                other = jnp.where(lane % nz == 0, read(floor), read(roof))
+                shift = LANES - nz if sign > 0 else nz
             else:
-                value = jnp.where(lane >= LANES - nz, pltpu.roll(other, LANES - nz - nz * chunk, 1), value)
-        elif t == 2 * len(against):
-            floor, roof = wall_pair(1, sign)
-            other = jnp.where(lane % nz == 0, read(floor), read(roof))
-            if sign > 0:
-                value = jnp.where(lane < nz, pltpu.roll(other, LANES - nz, 1), value)
-            else:
-                value = jnp.where(lane >= LANES - nz, pltpu.roll(other, nz, 1), value)
+                other = read(unit)
+                shift = half - nz * chunk if sign > 0 else LANES - nz - nz * chunk
+            spare = lane < nz if sign > 0 else lane >= LANES - nz
+            value = jnp.where(spare, pltpu.roll(other, shift, 1), value)
         store(len(along) + t, value)
 
 
 def unpack_columns(read, store, sign, lane, nz):
-    along, still, against = split_units(1, sign)
+    along, still, carried = message_plan(sign)
     for t, u in enumerate(along):
         store(u, read(t))
     base = len(along)
     for t, u in enumerate(still):
         store(u, read(base + t))
     half = LANES // 2
-    for t, u in enumerate(against):
-        first, second = read(base + 2 * t), read(base + 2 * t + 1)
+    for u in split_units(1, sign)[2]:
+        first, second = (read(base + carried.index((u, chunk))) for chunk in range(2))
         if sign > 0:
             value = jnp.where(lane < LANES - nz, pltpu.roll(first, half, 1), pltpu.roll(second, half + nz, 1))
         else:
             value = jnp.where(lane < nz, pltpu.roll(first, nz, 1), pltpu.roll(second, 2 * nz, 1))
         if u in wall_pair(1, sign):
-            walls = read(base + 2 * len(against))
+            walls = read(base + carried.index((None, 0)))
             if sign > 0:
                 value = jnp.where(lane < half, pltpu.roll(walls, nz, 1), value)
             else:
                 value = jnp.where(lane >= half, pltpu.roll(walls, LANES - nz, 1), value)
         store(u, value)
+
+
+def corner_plan(sign, sign_y):
+    along, still, _ = message_plan(sign_y)
+    units = list(along) + list(still)
+    plan, offset = [], 0
+    for t, u in enumerate(units):
+        depth = STEPS - 1 + sign * SPEED[u][0]
+        plan.append((t, STEPS - depth if sign > 0 else 0, depth, offset))
+        offset += depth
+    walls = tuple(units.index(u) for u in wall_pair(0, sign))
+    return plan, (offset, 1 if sign > 0 else 2), walls, -(-(offset + 1) // ROWS) * ROWS
 
 
 def relax(h, q, solid, inflow, emission, wind):
@@ -306,22 +327,49 @@
             pack_rows(lambda u, low, depth, c=c: one[u, c, low : low + depth, :], store, sign, first, height)
 
 
-def turn_corner(from_near, from_far, _, one, x_near, x_far, *, nz):
-    wide = one.shape[1]
-    extent = one.shape[2] - 2 * STEPS
+def turn_corner(y_near, y_far, x_near, x_far, *, nz):
+    extent = y_near.shape[1]
+    height = lane_index() % nz
+
+    def pack(sources, targets):
+        for side, (sign_y, source) in enumerate(zip((1, -1), sources)):
+            for sign, target, first in zip((1, -1), targets, (extent - STEPS, 0)):
+                plan, (offset, row), (floor, roof), _ = corner_plan(sign, sign_y)
+                for t, low, depth, at in plan:
+                    target[side, at : at + depth, :] = source[t, first + low : first + low + depth, :]
+                at = slice(first + row, first + row + 1)
+                target[side, offset : offset + 1, :] = jnp.where(
+                    height[:1] == 0, source[floor, at, :], source[roof, at, :]
+                )
+
+    by_side(
+        "gy",
+        lambda north, south: by_side("gx", lambda up, down: pack((south, north), (up, down)), x_near, x_far),
+        y_near,
+        y_far,
+    )
+
+
+def take_corners(one, near, far, stage, nz):
+    wide, extent = one.shape[1], one.shape[2] - 2 * STEPS
     lane = lane_index()
-    height = lane % nz
-
-    def unpack(north, south):
-        for sign, source, at in ((1, south, 0), (-1, north, wide - 1)):
-            for r in range(0, extent, ROWS):
-                def store(u, value, at=at, r=r):
-                    one[u, at, STEPS + r : STEPS + r + ROWS, :] = value
-
-                unpack_columns(lambda t, source=source, r=r: source[t, r : r + ROWS, :], store, sign, lane, nz)
-
-    by_side("gy", unpack, from_near, from_far)
-    by_side("gx", lambda up, down: pack_sides(one, (0, wide - 1), up, down, extent, height), x_near, x_far)
+
+    def lay(east, west):
+        for side, sign_y in enumerate((1, -1)):
+            for sign, source, first in ((1, west, 0), (-1, east, STEPS)):
+                plan, (offset, row), walls, _ = corner_plan(sign, sign_y)
+                for t, low, depth, at in plan:
+                    stage[side, t, first + low : first + low + depth, :] = source[side, at : at + depth, :]
+                for t in walls:
+                    stage[side, t, first + row : first + row + 1, :] = source[side, offset : offset + 1, :]
+
+    by_side("gx", lay, near, far)
+    for side, (sign_y, c) in enumerate(((1, 0), (-1, wide - 1))):
+        def store(u, value, c=c):
+            one[u, c, :STEPS, :] = value[:STEPS]
+            one[u, c, STEPS + extent :, :] = value[STEPS:]
+
+        unpack_columns(lambda t, side=side: stage[side, t, :, :], store, sign_y, lane, nz)
 
 
 class Mover:
@@ -471,13 +519,25 @@
             )
 
 
-def outer_centre(winds, *refs, nz):
+def outer_centre(winds, near, far, *refs, nz):
+    one = refs[5]
     block = Block(*refs[5:], winds, nz)
+    lane = lane_index()
+
+    def unpack(north, south):
+        for sign, source, c in ((1, south, 0), (-1, north, block.last)):
+            for r in range(0, block.extent, ROWS):
+                def store(u, value, c=c, r=r):
+                    one[u, c, STEPS + r : STEPS + r + ROWS, :] = value
+
+                unpack_columns(lambda t, source=source, r=r: source[t, r : r + ROWS, :], store, sign, lane, nz)
+
+    by_side("gy", unpack, near, far)
     block.outer(block.centre)
 
 
 def outer_seam(winds, near, far, *refs, nz):
-    one, two, three, four, done, flow_out, tracer_out, sems = refs[5:]
+    one, two, three, four, done, flow_out, tracer_out, stage, sems = refs[5:]
     block = Block(one, two, three, four, done, winds, nz)
     copies = []
 
@@ -492,8 +552,7 @@
 
     for j in range(1, block.tiles - 1):
         write_out(j)
-    columns = (0, block.last)
-    by_side("gx", lambda east, west: fill_rows(one, columns, west, east, block.extent), near, far)
+    take_corners(one, near, far, stage, nz)
     block.steps(
         lambda step: (0, 1, block.tiles, block.last) if step == 1 else (block.both, 1, block.tiles),
         lambda step: [block.seam(step)],
@@ -574,21 +633,24 @@
     x_near = swapped(x_near, "gx", 0)
     x_far = swapped(x_far, "gx", 1)
     state = run(lambda *refs: inner_centre(*refs, nz=nz), levels, (winds, one), aliases={1: 0})
-    one, corner_near, corner_far = run(
-        lambda *refs: turn_corner(*refs, nz=nz),
-        (first, vm(2, packed, LANES), vm(2, packed, LANES)),
-        (y_near, y_far, state[0]),
-        aliases={2: 0},
+    turned = corner_plan(1, 1)[3]
+    corner_near, corner_far = run(
+        lambda *refs: turn_corner(*refs, nz=nz), (vm(2, turned, LANES), vm(2, turned, LANES)), (y_near, y_far)
     )
     corner_near = swapped(corner_near, "gx", 0)
     corner_far = swapped(corner_far, "gx", 1)
     state = run(
+        lambda *refs: outer_centre(*refs, nz=nz),
+        levels,
+        (winds, y_near, y_far, *state),
+        aliases={3 + n: n for n in range(5)},
+    )
+    state = run(
         lambda *refs: inner_seam(*refs, nz=nz),
         levels,
-        (winds, x_near, x_far, one, *state[1:]),
+        (winds, x_near, x_far, *state),
         aliases={3 + n: n for n in range(5)},
     )
-    state = run(lambda *refs: outer_centre(*refs, nz=nz), levels, (winds, *state), aliases={1 + n: n for n in range(5)})
     out = run(
         lambda *refs: outer_seam(*refs, nz=nz),
         levels
@@ -598,7 +660,7 @@
         ),
         (winds, corner_near, corner_far, *state),
         out_specs=(close,) * 5 + (far, far),
-        scratch=[pltpu.SemaphoreType.DMA((2 * tiles,))],
+        scratch=[vm(2, messages, ROWS, LANES), pltpu.SemaphoreType.DMA((2 * tiles,))],
         aliases={3 + n: n for n in range(5)},
     )
     return out[5], out[6]

time: 20.5 us -> 21.6 us (1.054)
  waiting for transfers between devices: 1.34 us -> 2.32 us
    ppermute x6, waiting for transfers between devices: 1.34 us -> 2.32 us  [swapped(): return lax.ppermute(shard, axis, pairs)]
  transfers between devices with their start and end apart: 6 -> 6, of which waited for: 2 -> 2; matrix products, arithmetic and copies ran while one was open for 0% -> 0% of each run, Pallas kernels for 25% -> 24%
where the time goes in v4:
time: 21.6 us; the launch traced here: 21.4 us
  starting transfers between devices  10 us (46%)
  Pallas kernels  8.34 us (39%)
  waiting for transfers between devices  2.32 us (11%)
  between operations  0.73 us (3%)
    ppermute x6, starting transfers between devices, swapped(): return lax.ppermute(shard, axis, pairs)  10 us
    pallas_call x7, Pallas kernels, run(): pl.pallas_call(body, out_shape=out_shape, in_specs=specs, scratch_shapes=...  8.34 us
    ppermute x6, waiting for transfers between devices, swapped(): return lax.ppermute(shard, axis, pairs)  2.32 us
  transfers between devices with their start and end apart: 6, of which 2 were waited for; matrix products, arithmetic and copies ran while one was open for 0% of the time, Pallas kernels for 24%

profile of v4, /device:TPU:0, one launch (start us, length us, event | category | flops | bytes accessed | tf_op | source)
XLA Modules:
  0.0 21.4 jit_solution(14191999801236238077)
XLA Ops:
  0.6 1.4 %shard_map.77 = (f32[29,6,24,128]{3,2,1,0:T(8,128)S(1)}, f32[3,128]{1,0:T(4,128)S(1)}, f32[23,16,128]{2,1,0:T(8,128)S(1)}, f32[23,16,128]{2,1,0:T(8,128)S(1)}) custom-call(f32[19,16,512]{2,1,0:T(8,128)} %refs_0_.1, f32[7,16,512]{2,1,0:T(8,128)} %refs_1_.1, s32[16,512]{1,0:T(8,128)} %refs_2_.1, s32[16,512]{1,0:T(8,128)} %refs_3_.1, f32[3,32]{1,0:T(4,128)} %wind.1, ...), custom_call_target="tpu_custom_call" | custom-call | tf_op jit(solution)/shard_map/pallas_call | solution.py:603
  2.0 3.1 %collective-permute-start = (f32[23,16,128]{2,1,0:T(8,128)S(1)}, f32[23,16,128]{2,1,0:T(8,128)S(1)}, u32[]{:S(2)}, u32[]{:S(2)}) collective-permute-start(f32[23,16,128]{2,1,0:T(8,128)S(1)} %get-tuple-element.29), channel_id=1, source_target_pairs={{0,1},{1,0},{2,3},{3,2},{4,5},{5,4},{6,7},{7,6},{8,9},{9,8},{10,11... | collective-permute-start | bytes 565256 | tf_op jit(solution)/shard_map/ppermute | solution.py:571
  5.1 3.5 %collective-permute-start.1 = (f32[23,16,128]{2,1,0:T(8,128)S(1)}, f32[23,16,128]{2,1,0:T(8,128)S(1)}, u32[]{:S(2)}, u32[]{:S(2)}) collective-permute-start(f32[23,16,128]{2,1,0:T(8,128)S(1)} %get-tuple-element.30), channel_id=1, source_target_pairs={{1,2},{2,1},{3,4},{4,3},{5,6},{6,5},{7,0},{0,7},{9,10},{10,9},{11,... | collective-permute-start | bytes 565256 | tf_op jit(solution)/shard_map/ppermute | solution.py:571
  8.7 1.4 %shard_map.79 = (f32[29,6,24,128]{3,2,1,0:T(8,128)S(1)}, f32[4,88,128]{2,1,0:T(8,128)S(1)}, f32[4,88,128]{2,1,0:T(8,128)S(1)}) custom-call(f32[19,16,512]{2,1,0:T(8,128)} %refs_0_.1, f32[7,16,512]{2,1,0:T(8,128)} %refs_1_.1, s32[16,512]{1,0:T(8,128)} %refs_2_.1, s32[16,512]{1,0:T(8,128)} %refs_3_.1, ...), custom_call_target="tpu_custom_call", output_to_operand_aliasing={{0}: (6, {})} | custom-call | tf_op jit(solution)/shard_map/pallas_call | solution.py:603
  10.0 0.1 collective-permute-start.4
  10.1 1.6 %collective-permute-start.5 = (f32[4,88,128]{2,1,0:T(8,128)S(1)}, f32[4,88,128]{2,1,0:T(8,128)S(1)}, u32[]{:S(2)}, u32[]{:S(2)}) collective-permute-start(f32[4,88,128]{2,1,0:T(8,128)S(1)} %get-tuple-element.35), channel_id=1, source_target_pairs={{8,16},{16,8},{24,0},{0,24},{9,17},{17,9},{25,1},{1,25},{10,18},{1... | collective-permute-start | bytes 540680 | tf_op jit(solution)/shard_map/ppermute | solution.py:571
  11.7 1.4 %collective-permute-done.refs_0_.refs_1_ = f32[23,16,128]{2,1,0:T(8,128)S(1)} collective-permute-done((f32[23,16,128]{2,1,0:T(8,128)S(1)}, f32[23,16,128]{2,1,0:T(8,128)S(1)}, u32[]{:S(2)}, u32[]{:S(2)}) %collective-permute-start) | collective-permute-done | bytes 188448 | tf_op jit(solution)/shard_map/ppermute | solution.py:571
  13.1 0.9 %collective-permute-done.1.refs_1_.refs_2_ = f32[23,16,128]{2,1,0:T(8,128)S(1)} collective-permute-done((f32[23,16,128]{2,1,0:T(8,128)S(1)}, f32[23,16,128]{2,1,0:T(8,128)S(1)}, u32[]{:S(2)}, u32[]{:S(2)}) %collective-permute-start.1) | collective-permute-done | bytes 188448 | tf_op jit(solution)/shard_map/ppermute | solution.py:571
  14.0 0.1 collective-permute-start.2
  14.1 1.7 %collective-permute-start.3 = (f32[2,72,128]{2,1,0:T(8,128)S(1)}, f32[2,72,128]{2,1,0:T(8,128)S(1)}, u32[]{:S(2)}, u32[]{:S(2)}) collective-permute-start(f32[2,72,128]{2,1,0:T(8,128)S(1)} %get-tuple-element.32), channel_id=1, source_target_pairs={{8,16},{16,8},{24,0},{0,24},{9,17},{17,9},{25,1},{1,25},{10,18},{1... | collective-permute-start | bytes 221192 | tf_op jit(solution)/shard_map/ppermute | solution.py:571
  15.8 1.4 %shard_map.80 = (f32[29,6,24,128]{3,2,1,0:T(8,128)S(1)}, f32[26,6,24,128]{3,2,1,0:T(8,128)S(1)}, f32[26,7,24,128]{3,2,1,0:T(8,128)S(1)}, f32[26,7,24,128]{3,2,1,0:T(8,128)S(1)}, f32[26,4,16,128]{3,2,1,0:T(8,128)S(1)}) custom-call(f32[3,128]{1,0:T(4,128)S(1)} %get-tuple-element.28.refs_5_.refs_0_, ...), custom_call_target="tpu_custom_call", output_to_operand_aliasing={{0}: (1, {})} | custom-call | tf_op jit(solution)/shard_map/pallas_call | solution.py:603
  17.2 1.3 %shard_map.81 = (f32[29,6,24,128]{3,2,1,0:T(8,128)S(1)}, f32[26,6,24,128]{3,2,1,0:T(8,128)S(1)}, f32[26,7,24,128]{3,2,1,0:T(8,128)S(1)}, f32[26,7,24,128]{3,2,1,0:T(8,128)S(1)}, f32[26,4,16,128]{3,2,1,0:T(8,128)S(1)}) custom-call(f32[3,128]{1,0:T(4,128)S(1)} %get-tuple-element.28.refs_, ...), custom_call_target="tpu_custom_call", output_to_operand_aliasing={{0}: (3, {}), {1}: (4, {}), {2}: (5, {}), {3}: (6, {}), {4}... | custom-call | tf_op jit(solution)/shard_map/pallas_call | solution.py:603
  18.6 0.0 collective-permute-done.4.refs_1_
  18.6 0.0 collective-permute-done.5.refs_2_
  18.6 1.0 %shard_map.82 = (f32[29,6,24,128]{3,2,1,0:T(8,128)S(1)}, f32[26,6,24,128]{3,2,1,0:T(8,128)S(1)}, f32[26,7,24,128]{3,2,1,0:T(8,128)S(1)}, f32[26,7,24,128]{3,2,1,0:T(8,128)S(1)}, f32[26,4,16,128]{3,2,1,0:T(8,128)S(1)}) custom-call(f32[3,128]{1,0:T(4,128)S(1)} %get-tuple-element.28.refs_, ...), custom_call_target="tpu_custom_call", output_to_operand_aliasing={{0}: (3, {}), {1}: (4, {}), {2}: (5, {}), {3}: (6, {}), {4}... | custom-call | tf_op jit(solution)/shard_map/pallas_call | solution.py:603
  19.6 0.0 collective-permute-done.2.refs_1_
  19.7 0.0 collective-permute-done.3.refs_2_
  19.7 1.8 %shard_map.83 = (f32[29,6,24,128]{3,2,1,0:T(8,128)S(1)}, f32[26,6,24,128]{3,2,1,0:T(8,128)S(1)}, f32[26,7,24,128]{3,2,1,0:T(8,128)S(1)}, f32[26,7,24,128]{3,2,1,...) custom-call(f32[3,128]{1,0:T(4,128)S(1)} %get-tuple-element.28.refs_, ...), custom_call_target="tpu_custom_call", output_to_operand_aliasing={{0}: (3, {}), {1}: (4, {}), {2}: (5, {}), {3}: (6, {}), {4}... | custom-call | tf_op jit(solution)/shard_map/pallas_call | solution.py:603
  (1 shorter events, 0.0 us)
Async XLA Ops:
  2.0 11.1 %collective-permute-start = (f32[23,16,128]{2,1,0:T(8,128)S(1)}, f32[23,16,128]{2,1,0:T(8,128)S(1)}, u32[]{:S(2)}, u32[]{:S(2)}) collective-permute-start(f32[23,16,128]{2,1,0:T(8,128)S(1)} %get-tuple-element.29), channel_id=1, source_target_pairs={{0,1},{1,0},{2,3},{3,2},{4,5},{5,4},{6,7},{7,6},{8,9},{9,8},{10,11... | collective-permute-start | bytes 565256 | tf_op jit(solution)/shard_map/ppermute | solution.py:571
  5.1 8.9 %collective-permute-start.1 = (f32[23,16,128]{2,1,0:T(8,128)S(1)}, f32[23,16,128]{2,1,0:T(8,128)S(1)}, u32[]{:S(2)}, u32[]{:S(2)}) collective-permute-start(f32[23,16,128]{2,1,0:T(8,128)S(1)} %get-tuple-element.30), channel_id=1, source_target_pairs={{1,2},{2,1},{3,4},{4,3},{5,6},{6,5},{7,0},{0,7},{9,10},{10,9},{11,... | collective-permute-start | bytes 565256 | tf_op jit(solution)/shard_map/ppermute | solution.py:571
  10.0 8.6 %collective-permute-start.4 = (f32[4,88,128]{2,1,0:T(8,128)S(1)}, f32[4,88,128]{2,1,0:T(8,128)S(1)}, u32[]{:S(2)}, u32[]{:S(2)}) collective-permute-start(f32[4,88,128]{2,1,0:T(8,128)S(1)} %get-tuple-element.34), channel_id=1, source_target_pairs={{0,8},{8,0},{16,24},{24,16},{1,9},{9,1},{17,25},{25,17},{2,10},{10... | collective-permute-start | bytes 540680 | tf_op jit(solution)/shard_map/ppermute | solution.py:571
  10.1 8.5 %collective-permute-start.5 = (f32[4,88,128]{2,1,0:T(8,128)S(1)}, f32[4,88,128]{2,1,0:T(8,128)S(1)}, u32[]{:S(2)}, u32[]{:S(2)}) collective-permute-start(f32[4,88,128]{2,1,0:T(8,128)S(1)} %get-tuple-element.35), channel_id=1, source_target_pairs={{8,16},{16,8},{24,0},{0,24},{9,17},{17,9},{25,1},{1,25},{10,18},{1... | collective-permute-start | bytes 540680 | tf_op jit(solution)/shard_map/ppermute | solution.py:571
  14.0 5.6 %collective-permute-start.2 = (f32[2,72,128]{2,1,0:T(8,128)S(1)}, f32[2,72,128]{2,1,0:T(8,128)S(1)}, u32[]{:S(2)}, u32[]{:S(2)}) collective-permute-start(f32[2,72,128]{2,1,0:T(8,128)S(1)} %get-tuple-element.31), channel_id=1, source_target_pairs={{0,8},{8,0},{16,24},{24,16},{1,9},{9,1},{17,25},{25,17},{2,10},{10... | collective-permute-start | bytes 221192 | tf_op jit(solution)/shard_map/ppermute | solution.py:571
  14.1 5.5 %collective-permute-start.3 = (f32[2,72,128]{2,1,0:T(8,128)S(1)}, f32[2,72,128]{2,1,0:T(8,128)S(1)}, u32[]{:S(2)}, u32[]{:S(2)}) collective-permute-start(f32[2,72,128]{2,1,0:T(8,128)S(1)} %get-tuple-element.32), channel_id=1, source_target_pairs={{8,16},{16,8},{24,0},{0,24},{9,17},{17,9},{25,1},{1,25},{10,18},{1... | collective-permute-start | bytes 221192 | tf_op jit(solution)/shard_map/ppermute | solution.py:571

commit v5 on v4

--- a/solution.py
+++ b/solution.py
@@ -193,16 +193,29 @@
     density = jnp.where(inflow, 1.0, density)
     ux, uy, uz = (jnp.where(inflow, w, u) for w, u in zip(wind, (ux, uy, uz)))
     rest = 1.0 - rate
-    square = ux * ux + uy * uy + uz * uz
-    base = rate * (density - 1.5 * square)
-    linear = 3.0 * rate
-    quadratic = 4.5 * rate
+    uxx, uyy, uzz = ux * ux, uy * uy, uz * uz
+    base = rate * (density - 1.5 * (uxx + uyy + uzz))
+    linear, quadratic = 3.0 * rate, 4.5 * rate
+    lx, ly, lz = linear * ux, linear * uy, linear * uz
+    qx, qy, qz = quadratic * uxx, quadratic * uyy, quadratic * uzz
+    twice_x, twice_y = (linear * 3.0) * ux, (linear * 3.0) * uy
+    cxy, cxz, cyz = twice_x * uy, twice_x * uz, twice_y * uz
+    bx, by, bz = base + qx, base + qy, base + qz
+    bxy, bxz, byz = bx + qy, bx + qz, by + qz
     relaxed = [None] * 19
     relaxed[0] = jnp.where(solid, h[0], rest * h[0] + base)
-    along = {1: ux, 3: uy, 5: uz, 7: ux + uy, 9: ux - uy, 11: ux + uz, 13: ux - uz, 15: uy + uz, 17: uy - uz}
-    for k, speed in along.items():
-        even = base + quadratic * speed * speed
-        odd = linear * speed
+    parts = {
+        1: (bx, lx),
+        3: (by, ly),
+        5: (bz, lz),
+        7: (bxy + cxy, lx + ly),
+        9: (bxy - cxy, lx - ly),
+        11: (bxz + cxz, lx + lz),
+        13: (bxz - cxz, lx - lz),
+        15: (byz + cyz, ly + lz),
+        17: (byz - cyz, ly - lz),
+    }
+    for k, (even, odd) in parts.items():
         relaxed[k] = jnp.where(solid, h[k + 1], rest * h[k] + (even + odd))
         relaxed[k + 1] = jnp.where(solid, h[k], rest * h[k + 1] + (even - odd))
     return relaxed + traced

time: 21.6 us -> 21.4 us (level)
    pallas_call x7, Pallas kernels: 8.34 us -> 8.13 us  [run(): pl.pallas_call(body, out_shape=out_shape, in_specs=specs, scratch_shapes=...]
  transfers between devices with their start and end apart: 6 -> 6, of which waited for: 2 -> 2; matrix products, arithmetic and copies ran while one was open for 0% -> 0% of each run, Pallas kernels for 24% -> 23%
where the time goes in v5:
time: 21.4 us; the launch traced here: 21.2 us
  starting transfers between devices  10 us (47%)
  Pallas kernels  8.13 us (38%)
  waiting for transfers between devices  2.32 us (11%)
  between operations  0.72 us (3%)
    ppermute x6, starting transfers between devices, swapped(): return lax.ppermute(shard, axis, pairs)  10 us
    pallas_call x7, Pallas kernels, run(): pl.pallas_call(body, out_shape=out_shape, in_specs=specs, scratch_shapes=...  8.13 us
    ppermute x6, waiting for transfers between devices, swapped(): return lax.ppermute(shard, axis, pairs)  2.32 us
  transfers between devices with their start and end apart: 6, of which 2 were waited for; matrix products, arithmetic and copies ran while one was open for 0% of the time, Pallas kernels for 23%

profile of v5, /device:TPU:0, one launch (start us, length us, event | category | flops | bytes accessed | tf_op | source)
XLA Modules:
  0.0 21.2 jit_solution(12515716112279529859)
XLA Ops:
  0.6 1.4 %shard_map.77 = (f32[29,6,24,128]{3,2,1,0:T(8,128)S(1)}, f32[3,128]{1,0:T(4,128)S(1)}, f32[23,16,128]{2,1,0:T(8,128)S(1)}, f32[23,16,128]{2,1,0:T(8,128)S(1)}) custom-call(f32[19,16,512]{2,1,0:T(8,128)} %refs_0_.1, f32[7,16,512]{2,1,0:T(8,128)} %refs_1_.1, s32[16,512]{1,0:T(8,128)} %refs_2_.1, s32[16,512]{1,0:T(8,128)} %refs_3_.1, f32[3,32]{1,0:T(4,128)} %wind.1, ...), custom_call_target="tpu_custom_call" | custom-call | tf_op jit(solution)/shard_map/pallas_call | solution.py:616
  2.0 3.1 %collective-permute-start = (f32[23,16,128]{2,1,0:T(8,128)S(1)}, f32[23,16,128]{2,1,0:T(8,128)S(1)}, u32[]{:S(2)}, u32[]{:S(2)}) collective-permute-start(f32[23,16,128]{2,1,0:T(8,128)S(1)} %get-tuple-element.29), channel_id=1, source_target_pairs={{0,1},{1,0},{2,3},{3,2},{4,5},{5,4},{6,7},{7,6},{8,9},{9,8},{10,11... | collective-permute-start | bytes 565256 | tf_op jit(solution)/shard_map/ppermute | solution.py:584
  5.1 3.5 %collective-permute-start.1 = (f32[23,16,128]{2,1,0:T(8,128)S(1)}, f32[23,16,128]{2,1,0:T(8,128)S(1)}, u32[]{:S(2)}, u32[]{:S(2)}) collective-permute-start(f32[23,16,128]{2,1,0:T(8,128)S(1)} %get-tuple-element.30), channel_id=1, source_target_pairs={{1,2},{2,1},{3,4},{4,3},{5,6},{6,5},{7,0},{0,7},{9,10},{10,9},{11,... | collective-permute-start | bytes 565256 | tf_op jit(solution)/shard_map/ppermute | solution.py:584
  8.7 1.3 %shard_map.79 = (f32[29,6,24,128]{3,2,1,0:T(8,128)S(1)}, f32[4,88,128]{2,1,0:T(8,128)S(1)}, f32[4,88,128]{2,1,0:T(8,128)S(1)}) custom-call(f32[19,16,512]{2,1,0:T(8,128)} %refs_0_.1, f32[7,16,512]{2,1,0:T(8,128)} %refs_1_.1, s32[16,512]{1,0:T(8,128)} %refs_2_.1, s32[16,512]{1,0:T(8,128)} %refs_3_.1, ...), custom_call_target="tpu_custom_call", output_to_operand_aliasing={{0}: (6, {})} | custom-call | tf_op jit(solution)/shard_map/pallas_call | solution.py:616
  10.0 0.1 collective-permute-start.4
  10.1 1.6 %collective-permute-start.5 = (f32[4,88,128]{2,1,0:T(8,128)S(1)}, f32[4,88,128]{2,1,0:T(8,128)S(1)}, u32[]{:S(2)}, u32[]{:S(2)}) collective-permute-start(f32[4,88,128]{2,1,0:T(8,128)S(1)} %get-tuple-element.35), channel_id=1, source_target_pairs={{8,16},{16,8},{24,0},{0,24},{9,17},{17,9},{25,1},{1,25},{10,18},{1... | collective-permute-start | bytes 540680 | tf_op jit(solution)/shard_map/ppermute | solution.py:584
  11.7 1.5 %collective-permute-done.refs_0_.refs_1_ = f32[23,16,128]{2,1,0:T(8,128)S(1)} collective-permute-done((f32[23,16,128]{2,1,0:T(8,128)S(1)}, f32[23,16,128]{2,1,0:T(8,128)S(1)}, u32[]{:S(2)}, u32[]{:S(2)}) %collective-permute-start) | collective-permute-done | bytes 188448 | tf_op jit(solution)/shard_map/ppermute | solution.py:584
  13.1 0.9 %collective-permute-done.1.refs_1_.refs_2_ = f32[23,16,128]{2,1,0:T(8,128)S(1)} collective-permute-done((f32[23,16,128]{2,1,0:T(8,128)S(1)}, f32[23,16,128]{2,1,0:T(8,128)S(1)}, u32[]{:S(2)}, u32[]{:S(2)}) %collective-permute-start.1) | collective-permute-done | bytes 188448 | tf_op jit(solution)/shard_map/ppermute | solution.py:584
  14.0 0.1 collective-permute-start.2
  14.1 1.7 %collective-permute-start.3 = (f32[2,72,128]{2,1,0:T(8,128)S(1)}, f32[2,72,128]{2,1,0:T(8,128)S(1)}, u32[]{:S(2)}, u32[]{:S(2)}) collective-permute-start(f32[2,72,128]{2,1,0:T(8,128)S(1)} %get-tuple-element.32), channel_id=1, source_target_pairs={{8,16},{16,8},{24,0},{0,24},{9,17},{17,9},{25,1},{1,25},{10,18},{1... | collective-permute-start | bytes 221192 | tf_op jit(solution)/shard_map/ppermute | solution.py:584
  15.8 1.2 %shard_map.80 = (f32[29,6,24,128]{3,2,1,0:T(8,128)S(1)}, f32[26,6,24,128]{3,2,1,0:T(8,128)S(1)}, f32[26,7,24,128]{3,2,1,0:T(8,128)S(1)}, f32[26,7,24,128]{3,2,1,0:T(8,128)S(1)}, f32[26,4,16,128]{3,2,1,0:T(8,128)S(1)}) custom-call(f32[3,128]{1,0:T(4,128)S(1)} %get-tuple-element.28.refs_5_.refs_0_, ...), custom_call_target="tpu_custom_call", output_to_operand_aliasing={{0}: (1, {})} | custom-call | tf_op jit(solution)/shard_map/pallas_call | solution.py:616
  17.0 1.3 %shard_map.81 = (f32[29,6,24,128]{3,2,1,0:T(8,128)S(1)}, f32[26,6,24,128]{3,2,1,0:T(8,128)S(1)}, f32[26,7,24,128]{3,2,1,0:T(8,128)S(1)}, f32[26,7,24,128]{3,2,1,0:T(8,128)S(1)}, f32[26,4,16,128]{3,2,1,0:T(8,128)S(1)}) custom-call(f32[3,128]{1,0:T(4,128)S(1)} %get-tuple-element.28.refs_, ...), custom_call_target="tpu_custom_call", output_to_operand_aliasing={{0}: (3, {}), {1}: (4, {}), {2}: (5, {}), {3}: (6, {}), {4}... | custom-call | tf_op jit(solution)/shard_map/pallas_call | solution.py:616
  18.4 0.0 collective-permute-done.4.refs_1_
  18.4 0.0 collective-permute-done.5.refs_2_
  18.4 1.0 %shard_map.82 = (f32[29,6,24,128]{3,2,1,0:T(8,128)S(1)}, f32[26,6,24,128]{3,2,1,0:T(8,128)S(1)}, f32[26,7,24,128]{3,2,1,0:T(8,128)S(1)}, f32[26,7,24,128]{3,2,1,0:T(8,128)S(1)}, f32[26,4,16,128]{3,2,1,0:T(8,128)S(1)}) custom-call(f32[3,128]{1,0:T(4,128)S(1)} %get-tuple-element.28.refs_, ...), custom_call_target="tpu_custom_call", output_to_operand_aliasing={{0}: (3, {}), {1}: (4, {}), {2}: (5, {}), {3}: (6, {}), {4}... | custom-call | tf_op jit(solution)/shard_map/pallas_call | solution.py:616
  19.4 0.0 collective-permute-done.2.refs_1_
  19.4 0.0 collective-permute-done.3.refs_2_
  19.4 1.8 %shard_map.83 = (f32[29,6,24,128]{3,2,1,0:T(8,128)S(1)}, f32[26,6,24,128]{3,2,1,0:T(8,128)S(1)}, f32[26,7,24,128]{3,2,1,0:T(8,128)S(1)}, f32[26,7,24,128]{3,2,1,...) custom-call(f32[3,128]{1,0:T(4,128)S(1)} %get-tuple-element.28.refs_, ...), custom_call_target="tpu_custom_call", output_to_operand_aliasing={{0}: (3, {}), {1}: (4, {}), {2}: (5, {}), {3}: (6, {}), {4}... | custom-call | tf_op jit(solution)/shard_map/pallas_call | solution.py:616
  (1 shorter events, 0.0 us)
Async XLA Ops:
  2.0 11.1 %collective-permute-start = (f32[23,16,128]{2,1,0:T(8,128)S(1)}, f32[23,16,128]{2,1,0:T(8,128)S(1)}, u32[]{:S(2)}, u32[]{:S(2)}) collective-permute-start(f32[23,16,128]{2,1,0:T(8,128)S(1)} %get-tuple-element.29), channel_id=1, source_target_pairs={{0,1},{1,0},{2,3},{3,2},{4,5},{5,4},{6,7},{7,6},{8,9},{9,8},{10,11... | collective-permute-start | bytes 565256 | tf_op jit(solution)/shard_map/ppermute | solution.py:584
  5.1 8.9 %collective-permute-start.1 = (f32[23,16,128]{2,1,0:T(8,128)S(1)}, f32[23,16,128]{2,1,0:T(8,128)S(1)}, u32[]{:S(2)}, u32[]{:S(2)}) collective-permute-start(f32[23,16,128]{2,1,0:T(8,128)S(1)} %get-tuple-element.30), channel_id=1, source_target_pairs={{1,2},{2,1},{3,4},{4,3},{5,6},{6,5},{7,0},{0,7},{9,10},{10,9},{11,... | collective-permute-start | bytes 565256 | tf_op jit(solution)/shard_map/ppermute | solution.py:584
  10.0 8.4 %collective-permute-start.4 = (f32[4,88,128]{2,1,0:T(8,128)S(1)}, f32[4,88,128]{2,1,0:T(8,128)S(1)}, u32[]{:S(2)}, u32[]{:S(2)}) collective-permute-start(f32[4,88,128]{2,1,0:T(8,128)S(1)} %get-tuple-element.34), channel_id=1, source_target_pairs={{0,8},{8,0},{16,24},{24,16},{1,9},{9,1},{17,25},{25,17},{2,10},{10... | collective-permute-start | bytes 540680 | tf_op jit(solution)/shard_map/ppermute | solution.py:584
  10.1 8.3 %collective-permute-start.5 = (f32[4,88,128]{2,1,0:T(8,128)S(1)}, f32[4,88,128]{2,1,0:T(8,128)S(1)}, u32[]{:S(2)}, u32[]{:S(2)}) collective-permute-start(f32[4,88,128]{2,1,0:T(8,128)S(1)} %get-tuple-element.35), channel_id=1, source_target_pairs={{8,16},{16,8},{24,0},{0,24},{9,17},{17,9},{25,1},{1,25},{10,18},{1... | collective-permute-start | bytes 540680 | tf_op jit(solution)/shard_map/ppermute | solution.py:584
  14.0 5.4 %collective-permute-start.2 = (f32[2,72,128]{2,1,0:T(8,128)S(1)}, f32[2,72,128]{2,1,0:T(8,128)S(1)}, u32[]{:S(2)}, u32[]{:S(2)}) collective-permute-start(f32[2,72,128]{2,1,0:T(8,128)S(1)} %get-tuple-element.31), channel_id=1, source_target_pairs={{0,8},{8,0},{16,24},{24,16},{1,9},{9,1},{17,25},{25,17},{2,10},{10... | collective-permute-start | bytes 221192 | tf_op jit(solution)/shard_map/ppermute | solution.py:584
  14.1 5.3 %collective-permute-start.3 = (f32[2,72,128]{2,1,0:T(8,128)S(1)}, f32[2,72,128]{2,1,0:T(8,128)S(1)}, u32[]{:S(2)}, u32[]{:S(2)}) collective-permute-start(f32[2,72,128]{2,1,0:T(8,128)S(1)} %get-tuple-element.32), channel_id=1, source_target_pairs={{8,16},{16,8},{24,0},{0,24},{9,17},{17,9},{25,1},{1,25},{10,18},{1... | collective-permute-start | bytes 221192 | tf_op jit(solution)/shard_map/ppermute | solution.py:584
